TPU v7x, 32 devices: a whole 2x2x4 slice. The times are simulated.
32 devices in a mesh: pose: 16 (over z, y, x), chan: 2 (over core).
Axes of the slice: x: 2, y: 2, z: 4, core: 2. Of those that a mesh axis runs over, the one named last changes fastest.
Arguments:
- atom_type: int32 [16, 2304], P('pose'), may hold values from 0 to 27
- occupancy: int32 [16, 2304], P('pose'), may hold values from 0 to 3
- atom_embed: bfloat16 [28, 128], replicated, may hold values from -6 to 6
- conv1_weight: bfloat16 [27, 128, 256], replicated, may hold values from -0.109375 to 0.109375
- conv1_bias: float32 [256], replicated, may hold values from -3 to 3
- conv2_weight: bfloat16 [27, 256, 128], replicated, may hold values from -0.078125 to 0.078125
- conv2_bias: float32 [128], replicated, may hold values from -3 to 3
- head_weight: float32 [128, 2304], P('chan'), may hold values from -0.0029296875 to 0.0029296875
Outputs:
- plane_scores: float32 [16], P('pose')
- scores: float32 [1], replicated
All inputs are finite; a program needn't handle non-finite values.
Results may differ from a plain program's by a relative error of at most 0.0057.
Values may be sent and summed in bfloat16 or wider, within the bound.
No kernel may reach another device: no remote copies, remote signals or barrier semaphores. Data moves between devices by JAX's collectives and lax.ppermute only.
A program may use at most 64 MiB of HBM per device.

v0:
```python
import jax
import jax.numpy as jnp
from jax import lax
from jax.sharding import PartitionSpec as P

SIDE = 48
XPLANES = 16


stencil_offsets = [
    (shift_x, shift_y, shift_z)
    for shift_x in (-1, 0, 1)
    for shift_y in (-1, 0, 1)
    for shift_z in (-1, 0, 1)
]


def passed_along(array, axis, by):
    devices = lax.axis_size(axis)
    pairs = [(i, i + by) for i in range(devices) if 0 <= i + by < devices]
    return lax.ppermute(array, axis, pairs)


def plane_shift(grid_field, shift_y, shift_z, grid_side):
    cell_count = grid_field.shape[-1]
    reach_cells = grid_side + 1
    flat_step = shift_y * grid_side + shift_z
    widths = [(0, 0)] * (grid_field.ndim - 1) + [(reach_cells, reach_cells)]
    padded = jnp.pad(grid_field, widths)
    shifted = lax.slice_in_dim(
        padded,
        reach_cells + flat_step,
        reach_cells + flat_step + cell_count,
        axis=grid_field.ndim - 1,
    )
    positions = jnp.arange(cell_count, dtype=jnp.int32)
    coord_y = positions // grid_side + shift_y
    coord_z = positions % grid_side + shift_z
    inside = (coord_y >= 0) & (coord_y < grid_side) & (coord_z >= 0) & (coord_z < grid_side)
    return jnp.where(inside, shifted, jnp.zeros_like(shifted))


def convolve(padded, weight_taps, plane_count, grid_side):
    in_width = padded.shape[0]
    running = jnp.zeros((weight_taps.shape[2], plane_count * padded.shape[2]), jnp.float32)
    for offset_index, offset_item in enumerate(stencil_offsets):
        window = lax.slice_in_dim(
            padded, 1 + offset_item[0], 1 + offset_item[0] + plane_count, axis=1
        )
        shifted = plane_shift(window, offset_item[1], offset_item[2], grid_side).reshape(
            in_width, -1
        )
        running = running + jnp.dot(
            weight_taps[offset_index].T, shifted, preferred_element_type=jnp.float32
        )
    return running


def embed_cells(atom_embed, types, counts):
    type_table = (
        types[None, :, :] == jnp.arange(atom_embed.shape[0], dtype=jnp.int32)[:, None, None]
    ).astype(jnp.bfloat16)
    mixed = jnp.einsum("tc,tpv->cpv", atom_embed, type_table, preferred_element_type=jnp.float32)
    return (mixed * counts.astype(jnp.float32)[None, :, :]).astype(jnp.bfloat16)


def on_device(
    atom_type,
    occupancy,
    atom_embed,
    conv1_weight,
    conv1_bias,
    conv2_weight,
    conv2_bias,
    head_weight,
):
    chan_count = lax.axis_size("chan")
    chan_rank = lax.axis_index("chan")
    pose_count = lax.axis_size("pose")
    plane_count = atom_type.shape[0]
    cell_count = atom_type.shape[1]
    group_size = XPLANES // plane_count
    pose_total = pose_count // group_size
    mid_width = conv1_weight.shape[2]
    out_width = conv2_weight.shape[2]
    mid_share = mid_width // chan_count
    out_share = out_width // chan_count
    first_bias = lax.dynamic_slice_in_dim(conv1_bias, chan_rank * mid_share, mid_share, 0)
    second_bias = lax.dynamic_slice_in_dim(conv2_bias, chan_rank * out_share, out_share, 0)
    first_own = lax.dynamic_slice_in_dim(conv1_weight, chan_rank * mid_share, mid_share, 2)
    features = embed_cells(atom_embed, atom_type, occupancy)
    lower_rim = passed_along(features, "pose", pose_total)
    upper_rim = passed_along(features, "pose", -pose_total)
    padded = jnp.concatenate([lower_rim, features, upper_rim], axis=1)
    first_sum = convolve(padded, first_own, plane_count, SIDE)
    hidden = (
        jnp.maximum(first_sum + first_bias[:, None], 0.0)
        .astype(jnp.bfloat16)
        .reshape(mid_share, plane_count, cell_count)
    )
    lower_rim = passed_along(hidden, "pose", pose_total)
    upper_rim = passed_along(hidden, "pose", -pose_total)
    padded_own = jnp.concatenate([lower_rim, hidden, upper_rim], axis=1)
    input_rows = lax.dynamic_slice_in_dim(conv2_weight, chan_rank * mid_share, mid_share, 1)
    second_sum = lax.psum_scatter(
        convolve(padded_own, input_rows, plane_count, SIDE), "chan", scatter_dimension=0, tiled=True
    )
    mapped = jnp.maximum(second_sum + second_bias[:, None], 0.0).reshape(
        out_share, plane_count, cell_count
    )
    plane_terms = jnp.sum(mapped * head_weight[:, None, :], axis=(0, 2))
    plane_scores = lax.psum(plane_terms, "chan")
    every_plane = lax.all_gather(plane_scores, "pose", axis=0, tiled=True)
    scores = jnp.sum(every_plane.reshape(group_size, pose_total, plane_count), axis=(0, 2))
    return (plane_scores, scores)


def solution(mesh):
    return jax.shard_map(
        on_device,
        mesh=mesh,
        in_specs=(P("pose", None), P("pose", None), P(), P(), P(), P(), P(), P("chan", None)),
        out_specs=(P("pose"), P()),
        check_vma=False,
    )
```

profile of v0, /device:TPU:0, one launch (start us, length us, event | category | flops | bytes accessed | tf_op | source)
XLA Modules:
  0.0 166.7 jit_solution(4972470235952251231)
XLA Ops:
  7.2 0.9 convert_reduce_fusion
  8.1 0.7 reduce.5
  8.8 1.4 fusion.7
  10.2 4.9 %collective-permute-start = (bf16[128,1,2304]{0,2,1:T(8,128)(2,1)S(1)}, bf16[128,1,2304]{0,2,1:T(8,128)(2,1)S(1)}, u32[]{:S(2)}, u32[]{:S(2)}) collective-permute-start(bf16[128,1,2304]{0,2,1:T(8,128)(2,1)S(1)} %bitcast.328), channel_id=1, source_target_pairs={{0,2},{2,4},{4,6},{6,8},{8,10},{10,12},{12,14},{14,16},{16,18},{18... | collective-permute-start | bytes 1769480 | tf_op jit(solution)/shard_map/ppermute | solution.py:21
  15.1 1.3 collective-permute-start.1
  16.4 0.8 dynamic_slice.14
  17.3 23.0 %collective-permute-done = bf16[128,1,2304]{0,2,1:T(8,128)(2,1)S(1)} collective-permute-done((bf16[128,1,2304]{0,2,1:T(8,128)(2,1)S(1)}, bf16[128,1,2304]{0,2,1:T(8,128)(2,1)S(1)}, u32[]{:S(2)}, u32[]{:S(2)}) %collective-permute-start) | collective-permute-done | bytes 589856 | tf_op jit(solution)/shard_map/ppermute | solution.py:21
  40.8 0.5 convolution_add_fusion.23
  41.3 0.5 fusion.58
  42.3 0.5 convolution_add_fusion.21
  42.8 0.5 fusion.3
  43.3 0.5 convolution_add_fusion.19
  43.8 0.5 convolution_add_fusion.18
  44.8 0.5 convolution_add_fusion.16
  46.3 0.5 convolution_add_fusion.13
  46.8 0.5 convolution_add_fusion.12
  47.3 0.5 convolution_add_fusion.11
  47.8 0.5 convolution_add_fusion.10
  48.3 0.5 convolution_add_fusion.9
  49.3 0.5 fusion.40
  49.8 0.5 convolution_add_fusion.7
  51.3 0.5 convolution_add_fusion.4
  51.8 0.5 fusion.2
  52.3 0.5 convolution_add_fusion.2
  52.8 0.5 convolution_add_fusion.1
  53.3 1.5 fusion.6
  54.8 4.4 %collective-permute-start.2 = (bf16[128,1,2304]{0,2,1:T(8,128)(2,1)S(1)}, bf16[128,1,2304]{0,2,1:T(8,128)(2,1)S(1)}, u32[]{:S(2)}, u32[]{:S(2)}) collective-permute-start(bf16[128,1,2304]{0,2,1:T(8,128)(2,1)S(1)} %bitcast.338), channel_id=1, source_target_pairs={{0,2},{2,4},{4,6},{6,8},{8,10},{10,12},{12,14},{14,16},{16,18},{18... | collective-permute-start | bytes 1769480 | tf_op jit(solution)/shard_map/ppermute | solution.py:21
  59.3 1.5 collective-permute-start.3
  60.7 22.8 %collective-permute-done.2 = bf16[128,1,2304]{0,2,1:T(8,128)(2,1)S(1)} collective-permute-done((bf16[128,1,2304]{0,2,1:T(8,128)(2,1)S(1)}, bf16[128,1,2304]{0,2,1:T(8,128)(2,1)S(1)}, u32[]{:S(2)}, u32[]{:S(2)}) %collective-permute-start.2) | collective-permute-done | bytes 589856 | tf_op jit(solution)/shard_map/ppermute | solution.py:21
  83.6 0.6 fusion.34
  84.2 0.6 fusion.29
  84.8 0.6 convolution_add_fusion.47
  85.5 0.7 convolution_add_fusion.46
  86.1 0.6 convolution_add_fusion.45
  86.8 0.7 fusion.5
  87.4 0.6 convolution_add_fusion.43
  88.1 0.6 convolution_add_fusion.42
  88.7 0.6 convolution_add_fusion.41
  89.3 0.6 convolution_add_fusion.40
  90.0 0.6 convolution_add_fusion.39
  90.6 0.7 convolution_add_fusion.38
  91.3 0.6 convolution_add_fusion.37
  91.9 0.6 convolution_add_fusion.36
  92.6 0.7 convolution_add_fusion.35
  93.2 0.6 convolution_add_fusion.34
  93.9 0.6 convolution_add_fusion.33
  94.5 0.6 convolution_add_fusion.32
  95.2 0.6 fusion.11
  95.8 0.6 convolution_add_fusion.31
  96.4 0.6 convolution_add_fusion.30
  97.1 0.6 convolution_add_fusion.29
  97.7 0.8 convolution_add_fusion.28
  98.6 0.7 fusion.4
  99.2 0.6 convolution_add_fusion.26
  99.9 0.6 convolution_add_fusion.25
  100.5 2.4 %convolution_add_fusion.24 = f32[128,2304]{1,0:T(8,128)} fusion(f32[128,2304]{1,0:T(8,128)S(1)} %convolution_add_fusion.25, pred[2304]{0:T(1024)(128)(4,1)S(1)} %get-tuple-element.2, bf16[128,1,2304]{0,2,1:T(8,128)(2,1)S(1)} %collective-permute-done.3, bf16[27,256,128]{2,1,0:T(8,128)(2,1)S(1)} %copy-done.3, s32[]{:T(128)S(6)} %add.723, s32[]{:T(128)S(6)} %select_n.556), kind=kOutput, calls=%fused_computation.28 | convolution fusion | flops 76087296 | bytes 2984968 | tf_op jit(solution)/shard_map/dot_general | solution.py:53
  103.0 0.6 copy-done.4
  103.6 0.6 dynamic-slice
  104.3 6.6 %reduce-scatter.2.cloned.1.call-done = f32[64,2304]{1,0:T(8,128)} async-done(((f32[128,2304]{1,0:T(8,128)}), f32[64,2304]{1,0:T(8,128)}) %reduce-scatter.2.cloned.1.call-update) | async-done | bytes 589840 | tf_op jit(solution)/shard_map/reduce_scatter | solution.py:105
  110.9 1.9 %multiply_reduce_fusion = f32[]{:T(128)} fusion(f32[64,2304]{1,0:T(8,128)S(1)} %copy-done.2, f32[64,2304]{1,0:T(8,128)} %reduce-scatter.2.cloned.1.call-done, f32[64]{0:T(128)S(1)} %dynamic_slice.15), kind=kLoop, calls=%fused_computation.116 | loop fusion | flops 589823 | bytes 1179908 | tf_op jit(solution)/shard_map/reduce_sum | solution.py:111
  112.8 3.1 %psum.7 = f32[1]{0:T(128)} all-reduce(f32[1]{0:T(128)} %bitcast.110), channel_id=1, replica_groups=mesh['pose'=16,'chan'=2] {'chan'}, use_global_device_ids=true, to_apply=%region_2.3 | all-reduce | flops 1 | bytes 8 | tf_op jit(solution)/shard_map/psum | solution.py:112
  115.8 1.4 dynamic-update-slice
  117.2 42.0 %all-reduce.6 = f32[16]{0:T(128)S(1)} all-reduce(f32[16]{0:T(128)S(1)} %dynamic-update-slice), channel_id=1, replica_groups=mesh['pose'=16,'chan'=2] {'pose'}, use_global_device_ids=true, to_apply=%add.6 | all-reduce | flops 16 | bytes 128
  159.3 0.6 reduce_sum.24
  (30 shorter events, 4.2 us)
Async XLA Ops:
  7.2 33.1 %copy-start = (bf16[27,128,256]{2,1,0:T(8,128)(2,1)S(1)}, bf16[27,128,256]{2,1,0:T(8,128)(2,1)}, u32[]{:S(2)}) copy-start(bf16[27,128,256]{2,1,0:T(8,128)(2,1)} %param.11) | copy-start | bytes 5308420
  7.2 103.7 %reduce-scatter.2.cloned.1.call-start = ((), (), s32[]{:S(2)}) async-start(), calls=%async_computation.1 | async-start | bytes 1769472 | tf_op jit(solution)/shard_map/reduce_scatter | solution.py:105
  10.2 30.1 %collective-permute-start = (bf16[128,1,2304]{0,2,1:T(8,128)(2,1)S(1)}, bf16[128,1,2304]{0,2,1:T(8,128)(2,1)S(1)}, u32[]{:S(2)}, u32[]{:S(2)}) collective-permute-start(bf16[128,1,2304]{0,2,1:T(8,128)(2,1)S(1)} %bitcast.328), channel_id=1, source_target_pairs={{0,2},{2,4},{4,6},{6,8},{8,10},{10,12},{12,14},{14,16},{16,18},{18... | collective-permute-start | bytes 1769480 | tf_op jit(solution)/shard_map/ppermute | solution.py:21
  15.1 34.2 %collective-permute-start.1 = (bf16[128,1,2304]{0,2,1:T(8,128)(2,1)S(1)}, bf16[128,1,2304]{0,2,1:T(8,128)(2,1)S(1)}, u32[]{:S(2)}, u32[]{:S(2)}) collective-permute-start(bf16[128,1,2304]{0,2,1:T(8,128)(2,1)S(1)} %bitcast.329), channel_id=1, source_target_pairs={{2,0},{4,2},{6,4},{8,6},{10,8},{12,10},{14,12},{16,14},{18,16},{20... | collective-permute-start | bytes 1769480 | tf_op jit(solution)/shard_map/ppermute | solution.py:21
  53.3 30.3 %copy-start.3 = (bf16[27,256,128]{2,1,0:T(8,128)(2,1)S(1)}, bf16[27,256,128]{2,1,0:T(8,128)(2,1)}, u32[]{:S(2)}) copy-start(bf16[27,256,128]{2,1,0:T(8,128)(2,1)} %param.13) | copy-start | bytes 5308420
  54.8 28.7 %collective-permute-start.2 = (bf16[128,1,2304]{0,2,1:T(8,128)(2,1)S(1)}, bf16[128,1,2304]{0,2,1:T(8,128)(2,1)S(1)}, u32[]{:S(2)}, u32[]{:S(2)}) collective-permute-start(bf16[128,1,2304]{0,2,1:T(8,128)(2,1)S(1)} %bitcast.338), channel_id=1, source_target_pairs={{0,2},{2,4},{4,6},{6,8},{8,10},{10,12},{12,14},{14,16},{16,18},{18... | collective-permute-start | bytes 1769480 | tf_op jit(solution)/shard_map/ppermute | solution.py:21
  59.3 35.9 %collective-permute-start.3 = (bf16[128,1,2304]{0,2,1:T(8,128)(2,1)S(1)}, bf16[128,1,2304]{0,2,1:T(8,128)(2,1)S(1)}, u32[]{:S(2)}, u32[]{:S(2)}) collective-permute-start(bf16[128,1,2304]{0,2,1:T(8,128)(2,1)S(1)} %bitcast.339), channel_id=1, source_target_pairs={{2,0},{4,2},{6,4},{8,6},{10,8},{12,10},{14,12},{16,14},{18,16},{20... | collective-permute-start | bytes 1769480 | tf_op jit(solution)/shard_map/ppermute | solution.py:21
  102.9 0.7 copy-start.4
  102.9 0.7 copy-start.5
  102.9 7.9 %copy-start.2 = (f32[64,2304]{1,0:T(8,128)S(1)}, f32[64,2304]{1,0:T(8,128)}, u32[]{:S(2)}) copy-start(f32[64,2304]{1,0:T(8,128)} %param.15) | copy-start | bytes 1769476
  102.9 57.0 %copy-start.1 = (bf16[27,128,256]{2,1,0:T(8,128)(2,1)S(1)}, bf16[27,128,256]{2,1,0:T(8,128)(2,1)}, u32[]{:S(2)}) copy-start(bf16[27,128,256]{2,1,0:T(8,128)(2,1)} %param.11) | copy-start | bytes 5308420
Sparse Core Ops, SparseCore 0:
  103.1 7.7 reduce-scatter.1
where the time goes:
time: 167 us
  waiting for transfers between devices  52.4 us (31%)
  blocking collectives  45.1 us (27%)
  matrix products  34.9 us (21%)
  between operations  14.5 us (9%)
  starting transfers between devices  12.1 us (7%)
  other arithmetic  4.18 us (3%)
  local copies, waits for them, and re-layouts  3.47 us (2%)
    ppermute x4, waiting for transfers between devices, passed_along(): return lax.ppermute(array, axis, pairs)  45.8 us
    unnamed x1, blocking collectives  42 us
    dot_general x54, matrix products, convolve(): jnp.dot(weight_taps[offset_index].T, shifted, preferred_element_type=jnp....  33.5 us
    ppermute x4, starting transfers between devices, passed_along(): return lax.ppermute(array, axis, pairs)  12.1 us
    reduce_scatter x1, waiting for transfers between devices, on_device(): lax.psum_scatter(convolve(padded_own, input_rows, plane_count, SIDE), 'ch...  6.61 us
  transfers between devices with their start and end apart: 5, of which 3 were waited for; matrix products, arithmetic and copies ran while one was open for 13% of the time, Pallas kernels for 0%

commit v1 on v0

v1 whole, which is shorter than its diff:
```python
import functools

import jax
import jax.numpy as jnp
from jax import lax
from jax.experimental import pallas as pl
from jax.experimental.pallas import tpu as pltpu
from jax.sharding import PartitionSpec as P

SIDE = 48
XPLANES = 16
LANES = 128
TAPS = [(shift_y, shift_z) for shift_y in (-1, 0, 1) for shift_z in (-1, 0, 1)]

bf16 = jnp.bfloat16
f32 = jnp.float32
fp8 = jnp.float8_e4m3fn
REST_SCALE = 256.0


def fold_kernel(embed_ref, weight_ref, folded_ref, rest_ref, pair_ref, high_ref, low_ref):
    types = embed_ref.shape[0]
    embed = embed_ref[...].astype(f32)
    half = pair_ref.shape[0] // 2
    pair_ref[...] = jnp.zeros_like(pair_ref)
    pair_ref[:types, :] = embed
    pair_ref[half:half + types, :] = (3.0 * embed).astype(bf16).astype(f32)
    pair = pair_ref[...].astype(bf16)
    high_ref[...] = jnp.zeros_like(high_ref)
    low_ref[...] = jnp.zeros_like(low_ref)
    for dx in range(3):
        for tap in range(9):
            both = jnp.dot(pair, weight_ref[dx * 9 + tap], preferred_element_type=f32)
            once, thrice = both[:types, :], both[half:half + types, :]
            rounded = once.astype(bf16).astype(f32)
            first = 2 * types * tap
            high_ref[dx, types * tap:types * (tap + 1), :] = rounded
            low_ref[dx, first:first + types, :] = once - rounded
            low_ref[dx, first + types:first + 2 * types, :] = thrice - 3.0 * rounded
        folded_ref[dx] = high_ref[dx].astype(bf16)
        rest_ref[dx] = (low_ref[dx] * REST_SCALE).astype(fp8)


def fold_embedding(atom_embed, conv1_weight):
    types, width = atom_embed.shape
    mid = conv1_weight.shape[2]
    depth = round_up(9 * types, LANES)
    rest_depth = round_up(18 * types, LANES)
    return pl.pallas_call(
        fold_kernel,
        out_shape=(
            jax.ShapeDtypeStruct((3, depth, mid), bf16),
            jax.ShapeDtypeStruct((3, rest_depth, mid), fp8),
        ),
        scratch_shapes=[
            pltpu.VMEM((2 * round_up(types, 16), width), f32),
            pltpu.VMEM((3, depth, mid), f32),
            pltpu.VMEM((3, rest_depth, mid), f32),
        ],
        name="fold_embedding",
    )(atom_embed, conv1_weight)


def round_up(value, step):
    return -(-value // step) * step


def one_hot(rows, x, types, depth):
    width = rows[0][0].shape[1]
    sub = lax.broadcasted_iota(jnp.int32, (8, 1), 0)

    def spread(row):
        return jnp.broadcast_to(row[x:x + 1, :], (8, width))

    groups = []
    for first in range(0, depth, 8):
        low, high = first // types, (first + 7) // types
        if low >= len(rows):
            groups.append(jnp.zeros((8, width), f32))
            continue
        kind, count = spread(rows[low][0]), spread(rows[low][1])
        number = sub + (first - types * low)
        if high != low:
            own = sub < types * high - first
            number = jnp.where(own, number, number - types)
            if high < len(rows):
                kind = jnp.where(own, kind, spread(rows[high][0]))
                count = jnp.where(own, count, spread(rows[high][1]))
            else:
                count = jnp.where(own, count, 0.0)
        groups.append(jnp.where(kind == number, count, 0.0))
    return jnp.concatenate(groups, axis=0)


def main_kernel(
    chunk,
    pose_total,
    group_size,
    own_ref,
    near_ref,
    far_ref,
    head_own_hbm,
    head_far_hbm,
    folded_ref,
    rest_ref,
    bias1_ref,
    weight2_ref,
    bias2_ref,
    out_ref,
    planes_ref,
    onehot_ref,
    resthot_ref,
    hidden_ref,
    taps_ref,
    w2_ref,
    head_ref,
    sems,
):
    w2_copy = pltpu.make_async_copy(weight2_ref, w2_ref, sems.at[0])
    w2_copy.start()
    chan = lax.axis_index("chan")
    share = head_own_hbm.shape[0]
    head_cells = pl.ds(pl.multiple_of(chan * head_ref.shape[1], LANES), head_ref.shape[1])
    head_copies = [
        pltpu.make_async_copy(
            source.at[:, head_cells],
            head_ref.at[pl.ds(pl.multiple_of(part * share, share), share), :],
            sems.at[1 + number],
        )
        for number, (source, part) in enumerate(((head_own_hbm, chan), (head_far_hbm, 1 - chan)))
    ]
    for copy in head_copies:
        copy.start()
    block = lax.axis_index("pose") // pose_total
    plane_cells = own_ref.shape[1]
    half_cells = plane_cells // 2
    depth = folded_ref.shape[1]
    padded = hidden_ref.shape[1]
    types = 28
    window = half_cells + 3 * LANES

    planes_ref[...] = jnp.zeros_like(planes_ref)
    near, far = near_ref[...], far_ref[...]
    below = jnp.where(chan == 1, near, far)
    above = jnp.where(chan == 1, far, near)
    rows = [
        jnp.where(block >= 2, below[:, plane_cells:], 0),
        jnp.where(block >= 1, below[:, :plane_cells], 0),
        own_ref[...],
        jnp.where(block <= group_size - 2, above[:, :plane_cells], 0),
        jnp.where(block <= group_size - 3, above[:, plane_cells:], 0),
    ]
    for x in range(5):
        planes_ref[x:x + 1, LANES:LANES + plane_cells] = rows[x]
    start = pl.multiple_of(chan * half_cells, LANES)
    cells = planes_ref[:, pl.ds(start, window)]

    column = lax.rem(lax.broadcasted_iota(jnp.int32, (8, padded), 1), SIDE)
    plain, split = [], []
    for shift_y, shift_z in TAPS:
        first = LANES - SIDE + SIDE * shift_y + shift_z
        moved = cells[:, first:first + padded]
        inside = (column + shift_z >= 0) & (column + shift_z < SIDE)
        moved = jnp.where(inside, moved, 0)
        kind = lax.shift_right_logical(moved, 2)
        count = moved & 3
        plain.append((kind, count.astype(f32)))
        split.append(
            (
                jnp.where(count == 3, kind + types, kind),
                jnp.where(count == 3, 1, count).astype(f32),
            )
        )
    for x in range(5):
        onehot_ref[x] = one_hot(plain, x, types, depth).astype(bf16).T
        resthot_ref[x] = one_hot(split, x, 2 * types, rest_ref.shape[1]).astype(bf16).T.astype(fp8)

    bias1 = bias1_ref[...]
    for h in range(3):
        plane_ok = (block + (h - 1) >= 0) & (block + (h - 1) < group_size)
        for first in range(0, padded, chunk):
            total, rest = bias1, 0.0
            for dx in range(3):
                rest = rest + jnp.dot(
                    resthot_ref[h + dx, first:first + chunk, :],
                    rest_ref[dx],
                    preferred_element_type=f32,
                )
                total = total + jnp.dot(
                    onehot_ref[h + dx, first:first + chunk, :],
                    folded_ref[dx],
                    preferred_element_type=f32,
                )
            total = total + rest * (1.0 / REST_SCALE)
            index = first + lax.broadcasted_iota(jnp.int32, (chunk, 1), 0)
            lowest = jnp.where(plane_ok, jnp.where(chan == 0, SIDE, 0), padded)
            highest = jnp.where(chan == 0, half_cells + 2 * SIDE, half_cells + SIDE)
            inside = (index >= lowest) & (index < highest)
            hidden_ref[h, first:first + chunk, :] = jnp.where(
                inside, jnp.maximum(total, 0.0), 0.0
            ).astype(bf16)

    w2_copy.wait()
    out_width = weight2_ref.shape[2]
    for first in range(0, padded, chunk):
        total = None
        for h in range(3):
            taps = jnp.concatenate([w2_ref[h * 9 + tap] for tap in range(9)], axis=1)
            part = jnp.dot(
                hidden_ref[h, first:first + chunk, :], taps, preferred_element_type=f32
            )
            total = part if total is None else total + part
        for tap in range(9):
            taps_ref[tap, 8 + first:8 + first + chunk, :] = total[
                :, tap * out_width:(tap + 1) * out_width
            ]

    for copy in head_copies:
        copy.wait()
    bias2 = bias2_ref[...]
    running = jnp.zeros((8, out_width), f32)
    for first in range(0, half_cells, LANES):
        moved = []
        for shift_z in range(3):
            offset = 8 + first + shift_z - 1
            moved.append(
                taps_ref[shift_z, offset:offset + LANES, :]
                + taps_ref[3 + shift_z, offset + SIDE:offset + SIDE + LANES, :]
                + taps_ref[6 + shift_z, offset + 2 * SIDE:offset + 2 * SIDE + LANES, :]
            )
        column = lax.rem(first + lax.broadcasted_iota(jnp.int32, (LANES, 1), 0), SIDE)
        mapped = (
            bias2
            + moved[1]
            + jnp.where(column > 0, moved[0], 0.0)
            + jnp.where(column < SIDE - 1, moved[2], 0.0)
        )
        mapped = jnp.maximum(mapped, 0.0)
        scored = mapped * head_ref[:, first:first + LANES].T
        running = running + jnp.sum(scored.reshape(LANES // 8, 8, out_width), axis=0)
    out_ref[...] = jnp.broadcast_to(jnp.sum(running), out_ref.shape)


def rescore(own, near, far, head_own, head_far, folded, rest, bias1, weight2, bias2, copies):
    plane_cells = own.shape[1]
    half_cells = plane_cells // 2
    depth, mid = folded.shape[1:]
    width = weight2.shape[2]
    chunk = 256
    padded = round_up(half_cells + 2 * SIDE, chunk)
    pose_total = lax.axis_size("pose") // XPLANES
    vmem = pl.BlockSpec(memory_space=pltpu.VMEM)
    hbm = pl.BlockSpec(memory_space=pl.ANY)
    return pl.pallas_call(
        functools.partial(main_kernel, chunk, pose_total, XPLANES),
        out_shape=jax.ShapeDtypeStruct((copies, LANES), f32),
        in_specs=[vmem] * 3 + [hbm] * 2 + [vmem] * 3 + [hbm, vmem],
        out_specs=vmem,
        scratch_shapes=[
            pltpu.VMEM((8, plane_cells + 3 * LANES), jnp.int32),
            pltpu.VMEM((5, padded, depth), bf16),
            pltpu.VMEM((5, padded, rest.shape[1]), fp8),
            pltpu.VMEM((3, padded, mid), bf16),
            pltpu.VMEM((9, padded + 16, width), f32),
            pltpu.VMEM(weight2.shape, bf16),
            pltpu.VMEM((width, half_cells), f32),
            pltpu.SemaphoreType.DMA((3,)),
        ],
        name="rescore",
    )(own, near, far, head_own, head_far, folded, rest, bias1, weight2, bias2)


def final_kernel(pose_total, chan_count, parts_ref, plane_ref, scores_ref):
    parts = parts_ref[:, 0, :]
    pose = lax.broadcasted_iota(jnp.int32, parts.shape, 0) // chan_count
    first = lax.broadcasted_iota(jnp.int32, parts.shape, 1) == 0
    plane_ref[0] = jnp.sum(jnp.where(first & (pose == lax.axis_index("pose")), parts, 0.0))
    for p in range(pose_total):
        scores_ref[p] = jnp.sum(jnp.where(first & (lax.rem(pose, pose_total) == p), parts, 0.0))


def final_sums(parts, pose_total, chan_count):
    smem = pl.BlockSpec(memory_space=pltpu.SMEM)
    return pl.pallas_call(
        functools.partial(final_kernel, pose_total, chan_count),
        out_shape=(
            jax.ShapeDtypeStruct((1,), f32),
            jax.ShapeDtypeStruct((pose_total,), f32),
        ),
        out_specs=(smem, smem),
        name="final_sums",
    )(parts)


def on_device(
    atom_type,
    occupancy,
    atom_embed,
    conv1_weight,
    conv1_bias,
    conv2_weight,
    conv2_bias,
    head_weight,
):
    chan_count = lax.axis_size("chan")
    pose_count = lax.axis_size("pose")
    pose_total = pose_count // XPLANES
    swap = [(0, 1), (1, 0)]

    def fetch(steps):
        by = steps * pose_total
        pairs = []
        for i in range(pose_count):
            up = 2 * (i + by) + 1 if i + by < pose_count else 2 * i
            down = 2 * (i - by) if i >= by else 2 * i + 1
            pairs += [(2 * i, down), (2 * i + 1, up)]
        return lax.ppermute(code, ("pose", "chan"), pairs)

    code = atom_type * 4 + occupancy
    near = jnp.concatenate([fetch(1), fetch(2)], axis=1)
    folded, rest = fold_embedding(atom_embed, conv1_weight)
    far = lax.ppermute(near, "chan", swap)
    head_far = lax.ppermute(head_weight, "chan", swap)
    part = rescore(
        code,
        near,
        far,
        head_weight,
        head_far,
        folded,
        rest,
        conv1_bias[None, :],
        conv2_weight,
        conv2_bias[None, :],
        pose_count * chan_count,
    )
    parts = lax.all_to_all(part[:, None, :], ("pose", "chan"), 0, 0, tiled=True)
    return final_sums(parts, pose_total, chan_count)


def solution(mesh):
    return jax.shard_map(
        on_device,
        mesh=mesh,
        in_specs=(P("pose", None), P("pose", None), P(), P(), P(), P(), P(), P("chan", None)),
        out_specs=(P("pose"), P()),
        check_vma=False,
    )
```

time: 167 us -> 36.2 us (0.22)
  waiting for transfers between devices: 52.4 us -> 2.31 us
  matrix products: 34.9 us -> 0 us
  blocking collectives: 45.1 us -> 13 us
  Pallas kernels: 0 us -> 14.4 us
  between operations: 14.5 us -> 0.69 us
  starting transfers between devices: 12.1 us -> 3.82 us
  other arithmetic: 4.18 us -> 0.73 us
  local copies, waits for them, and re-layouts: 3.47 us -> 0.81 us
    ppermute x4, waiting for transfers between devices: 45.8 us -> 2.31 us  [the longest x2 2.3 us: fetch(): return lax.ppermute(code, ('pose', 'chan'), pairs)]
    unnamed x1 -> x0, blocking collectives: 42 us -> none
    dot_general x55 -> x0, matrix products: 34.9 us -> none  [the longest x54 33.5 us: convolve(): jnp.dot(weight_taps[offset_index].T, shifted, preferred_element_type=jnp....]
    pallas_call x0 -> x3, Pallas kernels: none -> 14.4 us  [the longest x1 10.1 us: rescore(): pl.pallas_call(functools.partial(main_kernel, chunk, pose_total, XPLANES)...]
    all_to_all x0 -> x1, blocking collectives: none -> 13 us  [on_device(): parts = lax.all_to_all(part[:, None, :], ('pose', 'chan'), 0, 0, tiled=True)]
    ppermute x4, starting transfers between devices: 12.1 us -> 3.82 us  [the longest x2 2.58 us: fetch(): return lax.ppermute(code, ('pose', 'chan'), pairs)]
    reduce_scatter x1 -> x0, waiting for transfers between devices: 6.61 us -> none  [on_device(): lax.psum_scatter(convolve(padded_own, input_rows, plane_count, SIDE), 'ch...]
    psum x1 -> x0, blocking collectives: 3.08 us -> none  [on_device(): plane_scores = lax.psum(plane_terms, 'chan')]
  transfers between devices with their start and end apart: 5 -> 4, of which waited for: 3 -> 2; matrix products, arithmetic and copies ran while one was open for 13% -> 0% of each run, Pallas kernels for 0% -> 8%
where the time goes in v1:
time: 36.2 us; the launch traced here: 35.8 us
  Pallas kernels  14.4 us (40%)
  blocking collectives  13 us (36%)
  starting transfers between devices  3.82 us (11%)
  waiting for transfers between devices  2.31 us (6%)
  local copies, waits for them, and re-layouts  0.81 us (2%)
  other arithmetic  0.73 us (2%)
  between operations  0.69 us (2%)
    all_to_all x1, blocking collectives, on_device(): parts = lax.all_to_all(part[:, None, :], ('pose', 'chan'), 0, 0, tiled=True)  13 us
    pallas_call x1, Pallas kernels, rescore(): pl.pallas_call(functools.partial(main_kernel, chunk, pose_total, XPLANES)...  10.1 us
    pallas_call x1, Pallas kernels, fold_embedding(): pl.pallas_call(fold_kernel, out_shape=(jax.ShapeDtypeStruct((3, depth, mi...  2.92 us
    ppermute x2, starting transfers between devices, fetch(): return lax.ppermute(code, ('pose', 'chan'), pairs)  2.58 us
    ppermute x2, waiting for transfers between devices, fetch(): return lax.ppermute(code, ('pose', 'chan'), pairs)  2.3 us
    pallas_call x1, Pallas kernels, final_sums(): pl.pallas_call(functools.partial(final_kernel, pose_total, chan_count), o...  1.38 us
    ppermute x1, starting transfers between devices, on_device(): head_far = lax.ppermute(head_weight, 'chan', swap)  1.24 us
    unnamed x9, local copies, waits for them, and re-layouts  0.81 us
  transfers between devices with their start and end apart: 4, of which 2 were waited for; matrix products, arithmetic and copies ran while one was open for 0% of the time, Pallas kernels for 8%

profile of v1, /device:TPU:0, one launch (start us, length us, event | category | flops | bytes accessed | tf_op | source)
XLA Modules:
  0.0 35.8 jit_solution(9217121600239533250)
XLA Ops:
  0.6 0.7 %multiply_add_fusion.own_ref = s32[1,2304]{1,0:T(1,128)S(1)} fusion(s32[1,2304]{1,0:T(1,128)} %param.9, s32[1,2304]{1,0:T(1,128)} %param.8), kind=kLoop, calls=%fused_computation | loop fusion | flops 4608 | bytes 27648 | tf_op jit(solution)/shard_map/add | solution.py:319
  1.4 0.0 copy-start.2
  1.4 0.5 %collective-permute-start = (s32[1,2304]{1,0:T(1,128)S(1)}, s32[1,2304]{1,0:T(1,128)S(1)}, u32[]{:S(2)}, u32[]{:S(2)}) collective-permute-start(s32[1,2304]{1,0:T(1,128)S(1)} %multiply_add_fusion.own_ref), channel_id=1, source_target_pairs={{0,1},{1,3},{2,0},{3,5},{4,2},{5,7},{6,4},{7,9},{8,6},{9,11},{10,8... | collective-permute-start | bytes 27656 | tf_op jit(solution)/shard_map/ppermute | solution.py:317
  1.9 2.0 %collective-permute-start.1 = (s32[1,2304]{1,0:T(1,128)S(1)}, s32[1,2304]{1,0:T(1,128)S(1)}, u32[]{:S(2)}, u32[]{:S(2)}) collective-permute-start(s32[1,2304]{1,0:T(1,128)S(1)} %multiply_add_fusion.own_ref), channel_id=1, source_target_pairs={{0,1},{1,5},{2,3},{3,7},{4,0},{5,9},{6,2},{7,11},{8,4},{9,13},{10,... | collective-permute-start | bytes 27656 | tf_op jit(solution)/shard_map/ppermute | solution.py:317
  4.0 1.2 %collective-permute-start.3 = (f32[64,2304]{1,0:T(8,128)}, f32[64,2304]{1,0:T(8,128)S(1)}, u32[]{:S(2)}, u32[]{:S(2)}) collective-permute-start(f32[64,2304]{1,0:T(8,128)} %head_own_hbm.1), channel_id=1, source_target_pairs={{0,1},{1,0},{2,3},{3,2},{4,5},{5,4},{6,7},{7,6},{8,9},{9,8},{10,11... | collective-permute-start | bytes 1769480 | tf_op jit(solution)/shard_map/ppermute | solution.py:323
  5.2 0.8 %collective-permute-done = s32[1,2304]{1,0:T(1,128)S(1)} collective-permute-done((s32[1,2304]{1,0:T(1,128)S(1)}, s32[1,2304]{1,0:T(1,128)S(1)}, u32[]{:S(2)}, u32[]{:S(2)}) %collective-permute-start) | collective-permute-done | bytes 9248 | tf_op jit(solution)/shard_map/ppermute | solution.py:317
  6.0 1.5 %collective-permute-done.1 = s32[1,2304]{1,0:T(1,128)S(1)} collective-permute-done((s32[1,2304]{1,0:T(1,128)S(1)}, s32[1,2304]{1,0:T(1,128)S(1)}, u32[]{:S(2)}, u32[]{:S(2)}) %collective-permute-start.1) | collective-permute-done | bytes 9248 | tf_op jit(solution)/shard_map/ppermute | solution.py:317
  7.5 0.0 copy-start.1
  7.5 0.0 collective-permute-start.2
  7.5 2.9 %fold_embedding.1 = (bf16[3,256,256]{2,1,0:T(8,128)(2,1)}, f8e4m3fn[3,512,256]{2,1,0:T(32,128)(4,1)}) custom-call(bf16[28,128]{1,0:T(8,128)(2,1)} %embed_ref.1, bf16[27,128,256]{2,1,0:T(8,128)(2,1)} %weight_ref.1), custom_call_target="tpu_custom_call" | custom-call | tf_op jit(solution)/shard_map/fold_embedding/pallas_call | solution.py:49
  10.4 0.0 collective-permute-done.2.far_ref
  10.4 0.0 copy-start.3
  10.4 0.0 collective-permute-done.3.head_far_hbm
  10.4 0.0 copy-start
  10.5 0.0 copy-done.2
  10.5 0.0 copy-done.1
  10.5 0.6 %copy-done.3 = s32[1,4608]{1,0:T(1,128)} copy-done((s32[1,4608]{1,0:T(1,128)}, s32[1,4608]{1,0:T(1,128)S(1)}, u32[]{:S(2)}) %copy-start.3) | copy-done | bytes 18456
  11.0 0.2 copy-done
  11.3 10.1 %rescore.1 = f32[32,128]{1,0:T(8,128)} custom-call(s32[1,2304]{1,0:T(1,128)} %copy-done.2, s32[1,4608]{1,0:T(1,128)} %copy-done.1, s32[1,4608]{1,0:T(1,128)} %copy-done.3, f32[64,2304]{1,0:T(8,128)} %head_own_hbm.1, f32[64,2304]{1,0:T(8,128)} %copy-done, bf16[3,256,256]{2,1,0:T(8,128)(2,1)} %get-tuple-element.4.folded_ref, ...), custom_call_target="tpu_custom_call" | custom-call | tf_op jit(solution)/shard_map/rescore/pallas_call | solution.py:254
  21.3 13.0 %all_to_all.5.parts_ref = f32[32,1,128]{2,1,0:T(1,128)} all-to-all(f32[32,1,128]{2,1,0:T(1,128)} %bitcast.3), channel_id=1, replica_groups=mesh['pose'=16,'chan'=2] {'pose','chan'}, dimensions={0} | all-to-all | bytes 32768 | tf_op jit(solution)/shard_map/all_to_all | solution.py:337
  34.4 1.4 %final_sums.1 = (f32[1]{0:T(128)}, f32[1]{0:T(128)}) custom-call(f32[32,1,128]{2,1,0:T(1,128)} %all_to_all.5.parts_ref), custom_call_target="tpu_custom_call" | custom-call | tf_op jit(solution)/shard_map/final_sums/pallas_call | solution.py:284
  (2 shorter events, 0.0 us)
Async XLA Ops:
  1.4 9.1 %copy-start.2 = (s32[1,2304]{1,0:T(1,128)}, s32[1,2304]{1,0:T(1,128)S(1)}, u32[]{:S(2)}) copy-start(s32[1,2304]{1,0:T(1,128)S(1)} %multiply_add_fusion.own_ref) | copy-start | bytes 27652
  1.4 4.7 %collective-permute-start = (s32[1,2304]{1,0:T(1,128)S(1)}, s32[1,2304]{1,0:T(1,128)S(1)}, u32[]{:S(2)}, u32[]{:S(2)}) collective-permute-start(s32[1,2304]{1,0:T(1,128)S(1)} %multiply_add_fusion.own_ref), channel_id=1, source_target_pairs={{0,1},{1,3},{2,0},{3,5},{4,2},{5,7},{6,4},{7,9},{8,6},{9,11},{10,8... | collective-permute-start | bytes 27656 | tf_op jit(solution)/shard_map/ppermute | solution.py:317
  1.9 5.6 %collective-permute-start.1 = (s32[1,2304]{1,0:T(1,128)S(1)}, s32[1,2304]{1,0:T(1,128)S(1)}, u32[]{:S(2)}, u32[]{:S(2)}) collective-permute-start(s32[1,2304]{1,0:T(1,128)S(1)} %multiply_add_fusion.own_ref), channel_id=1, source_target_pairs={{0,1},{1,5},{2,3},{3,7},{4,0},{5,9},{6,2},{7,11},{8,4},{9,13},{10,... | collective-permute-start | bytes 27656 | tf_op jit(solution)/shard_map/ppermute | solution.py:317
  4.0 6.5 %collective-permute-start.3 = (f32[64,2304]{1,0:T(8,128)}, f32[64,2304]{1,0:T(8,128)S(1)}, u32[]{:S(2)}, u32[]{:S(2)}) collective-permute-start(f32[64,2304]{1,0:T(8,128)} %head_own_hbm.1), channel_id=1, source_target_pairs={{0,1},{1,0},{2,3},{3,2},{4,5},{5,4},{6,7},{7,6},{8,9},{9,8},{10,11... | collective-permute-start | bytes 1769480 | tf_op jit(solution)/shard_map/ppermute | solution.py:323
  7.5 3.0 %copy-start.1 = (s32[1,4608]{1,0:T(1,128)}, s32[1,4608]{1,0:T(1,128)S(1)}, u32[]{:S(2)}) copy-start(s32[1,4608]{1,0:T(1,128)S(1)} %constant_dynamic-update-slice_fusion.near_ref) | copy-start | bytes 55300
  7.5 2.9 %collective-permute-start.2 = (s32[1,4608]{1,0:T(1,128)S(1)}, s32[1,4608]{1,0:T(1,128)S(1)}, u32[]{:S(2)}, u32[]{:S(2)}) collective-permute-start(s32[1,4608]{1,0:T(1,128)S(1)} %constant_dynamic-update-slice_fusion.near_ref), channel_id=1, source_target_pairs={{0,1},{1,0},{2,3},{3,2},{4,5},{5,4},{6,7},{7,6},{8,9},{9,8},{10,11... | collective-permute-start | bytes 55304 | tf_op jit(solution)/shard_map/ppermute | solution.py:322
  10.4 0.6 %copy-start.3 = (s32[1,4608]{1,0:T(1,128)}, s32[1,4608]{1,0:T(1,128)S(1)}, u32[]{:S(2)}) copy-start(s32[1,4608]{1,0:T(1,128)S(1)} %collective-permute-done.2.far_ref) | copy-start | bytes 55300
  10.4 0.8 %copy-start = (f32[64,2304]{1,0:T(8,128)}, f32[64,2304]{1,0:T(8,128)S(1)}, u32[]{:S(2)}) copy-start(f32[64,2304]{1,0:T(8,128)S(1)} %collective-permute-done.3.head_far_hbm) | copy-start | bytes 1769476

commit v2 on v1

--- a/solution.py
+++ b/solution.py
@@ -10,67 +10,67 @@
 SIDE = 48
 XPLANES = 16
 LANES = 128
+TILE = 256
+CHUNK = 256
 TAPS = [(shift_y, shift_z) for shift_y in (-1, 0, 1) for shift_z in (-1, 0, 1)]
 
 bf16 = jnp.bfloat16
 f32 = jnp.float32
-fp8 = jnp.float8_e4m3fn
-REST_SCALE = 256.0
-
-
-def fold_kernel(embed_ref, weight_ref, folded_ref, rest_ref, pair_ref, high_ref, low_ref):
+
+
+def in_vmem(array):
+    return pltpu.with_memory_space_constraint(array, pltpu.VMEM)
+
+
+def fold_kernel(embed_ref, weight_ref, folded_ref, pair_ref, rows_ref):
     types = embed_ref.shape[0]
     embed = embed_ref[...].astype(f32)
     half = pair_ref.shape[0] // 2
+    rest = round_up(9 * types, LANES)
     pair_ref[...] = jnp.zeros_like(pair_ref)
     pair_ref[:types, :] = embed
     pair_ref[half:half + types, :] = (3.0 * embed).astype(bf16).astype(f32)
     pair = pair_ref[...].astype(bf16)
-    high_ref[...] = jnp.zeros_like(high_ref)
-    low_ref[...] = jnp.zeros_like(low_ref)
+    rows_ref[...] = jnp.zeros_like(rows_ref)
     for dx in range(3):
         for tap in range(9):
             both = jnp.dot(pair, weight_ref[dx * 9 + tap], preferred_element_type=f32)
             once, thrice = both[:types, :], both[half:half + types, :]
             rounded = once.astype(bf16).astype(f32)
-            first = 2 * types * tap
-            high_ref[dx, types * tap:types * (tap + 1), :] = rounded
-            low_ref[dx, first:first + types, :] = once - rounded
-            low_ref[dx, first + types:first + 2 * types, :] = thrice - 3.0 * rounded
-        folded_ref[dx] = high_ref[dx].astype(bf16)
-        rest_ref[dx] = (low_ref[dx] * REST_SCALE).astype(fp8)
+            first = rest + 2 * types * tap
+            rows_ref[dx, types * tap:types * (tap + 1), :] = rounded
+            rows_ref[dx, first:first + types, :] = once - rounded
+            rows_ref[dx, first + types:first + 2 * types, :] = thrice - 3.0 * rounded
+        folded_ref[dx] = rows_ref[dx].astype(bf16)
 
 
 def fold_embedding(atom_embed, conv1_weight):
     types, width = atom_embed.shape
     mid = conv1_weight.shape[2]
-    depth = round_up(9 * types, LANES)
-    rest_depth = round_up(18 * types, LANES)
+    depth = round_up(9 * types, LANES) + round_up(18 * types, LANES)
     return pl.pallas_call(
         fold_kernel,
-        out_shape=(
-            jax.ShapeDtypeStruct((3, depth, mid), bf16),
-            jax.ShapeDtypeStruct((3, rest_depth, mid), fp8),
-        ),
+        out_shape=pltpu.VMEM((3, depth, mid), bf16),
         scratch_shapes=[
             pltpu.VMEM((2 * round_up(types, 16), width), f32),
             pltpu.VMEM((3, depth, mid), f32),
-            pltpu.VMEM((3, rest_depth, mid), f32),
         ],
+        compiler_params=pltpu.CompilerParams(vmem_limit_bytes=12 << 20),
         name="fold_embedding",
-    )(atom_embed, conv1_weight)
+    )(atom_embed, in_vmem(conv1_weight))
 
 
 def round_up(value, step):
     return -(-value // step) * step
 
 
-def one_hot(rows, x, types, depth):
-    width = rows[0][0].shape[1]
+def one_hot(rows, x, types, start):
+    width = TILE
+    depth = round_up(types * len(rows), LANES)
     sub = lax.broadcasted_iota(jnp.int32, (8, 1), 0)
 
     def spread(row):
-        return jnp.broadcast_to(row[x:x + 1, :], (8, width))
+        return jnp.broadcast_to(row[x:x + 1, start:start + width], (8, width))
 
     groups = []
     for first in range(0, depth, 8):
@@ -99,42 +99,23 @@
     own_ref,
     near_ref,
     far_ref,
-    head_own_hbm,
-    head_far_hbm,
+    head_own_ref,
+    head_far_ref,
     folded_ref,
-    rest_ref,
     bias1_ref,
     weight2_ref,
     bias2_ref,
     out_ref,
     planes_ref,
     onehot_ref,
-    resthot_ref,
     hidden_ref,
     taps_ref,
-    w2_ref,
     head_ref,
-    sems,
 ):
-    w2_copy = pltpu.make_async_copy(weight2_ref, w2_ref, sems.at[0])
-    w2_copy.start()
     chan = lax.axis_index("chan")
-    share = head_own_hbm.shape[0]
-    head_cells = pl.ds(pl.multiple_of(chan * head_ref.shape[1], LANES), head_ref.shape[1])
-    head_copies = [
-        pltpu.make_async_copy(
-            source.at[:, head_cells],
-            head_ref.at[pl.ds(pl.multiple_of(part * share, share), share), :],
-            sems.at[1 + number],
-        )
-        for number, (source, part) in enumerate(((head_own_hbm, chan), (head_far_hbm, 1 - chan)))
-    ]
-    for copy in head_copies:
-        copy.start()
     block = lax.axis_index("pose") // pose_total
     plane_cells = own_ref.shape[1]
     half_cells = plane_cells // 2
-    depth = folded_ref.shape[1]
     padded = hidden_ref.shape[1]
     types = 28
     window = half_cells + 3 * LANES
@@ -171,27 +152,26 @@
                 jnp.where(count == 3, 1, count).astype(f32),
             )
         )
-    for x in range(5):
-        onehot_ref[x] = one_hot(plain, x, types, depth).astype(bf16).T
-        resthot_ref[x] = one_hot(split, x, 2 * types, rest_ref.shape[1]).astype(bf16).T.astype(fp8)
-
     bias1 = bias1_ref[...]
-    for h in range(3):
-        plane_ok = (block + (h - 1) >= 0) & (block + (h - 1) < group_size)
-        for first in range(0, padded, chunk):
-            total, rest = bias1, 0.0
+    for first in range(0, padded, TILE):
+        for x in range(5):
+            onehot_ref[x, first:first + TILE, :] = jnp.concatenate(
+                [
+                    one_hot(plain, x, types, first),
+                    one_hot(split, x, 2 * types, first),
+                ],
+                axis=0,
+            ).astype(bf16).T
+    for first in range(0, padded, chunk):
+        for h in range(3):
+            plane_ok = (block + (h - 1) >= 0) & (block + (h - 1) < group_size)
+            total = bias1
             for dx in range(3):
-                rest = rest + jnp.dot(
-                    resthot_ref[h + dx, first:first + chunk, :],
-                    rest_ref[dx],
-                    preferred_element_type=f32,
-                )
                 total = total + jnp.dot(
                     onehot_ref[h + dx, first:first + chunk, :],
                     folded_ref[dx],
                     preferred_element_type=f32,
                 )
-            total = total + rest * (1.0 / REST_SCALE)
             index = first + lax.broadcasted_iota(jnp.int32, (chunk, 1), 0)
             lowest = jnp.where(plane_ok, jnp.where(chan == 0, SIDE, 0), padded)
             highest = jnp.where(chan == 0, half_cells + 2 * SIDE, half_cells + SIDE)
@@ -200,12 +180,11 @@
                 inside, jnp.maximum(total, 0.0), 0.0
             ).astype(bf16)
 
-    w2_copy.wait()
     out_width = weight2_ref.shape[2]
     for first in range(0, padded, chunk):
         total = None
         for h in range(3):
-            taps = jnp.concatenate([w2_ref[h * 9 + tap] for tap in range(9)], axis=1)
+            taps = jnp.concatenate([weight2_ref[h * 9 + tap] for tap in range(9)], axis=1)
             part = jnp.dot(
                 hidden_ref[h, first:first + chunk, :], taps, preferred_element_type=f32
             )
@@ -215,8 +194,12 @@
                 :, tap * out_width:(tap + 1) * out_width
             ]
 
-    for copy in head_copies:
-        copy.wait()
+    share = head_own_ref.shape[0]
+    head_cells = pl.ds(start, half_cells)
+    head_ref[pl.ds(pl.multiple_of(chan * share, share), share), :] = head_own_ref[:, head_cells]
+    head_ref[pl.ds(pl.multiple_of((1 - chan) * share, share), share), :] = head_far_ref[
+        :, head_cells
+    ]
     bias2 = bias2_ref[...]
     running = jnp.zeros((8, out_width), f32)
     for first in range(0, half_cells, LANES):
@@ -241,33 +224,40 @@
     out_ref[...] = jnp.broadcast_to(jnp.sum(running), out_ref.shape)
 
 
-def rescore(own, near, far, head_own, head_far, folded, rest, bias1, weight2, bias2, copies):
+def rescore(own, near, far, head_own, head_far, folded, bias1, weight2, bias2, copies):
     plane_cells = own.shape[1]
     half_cells = plane_cells // 2
     depth, mid = folded.shape[1:]
     width = weight2.shape[2]
-    chunk = 256
-    padded = round_up(half_cells + 2 * SIDE, chunk)
+    chunk = CHUNK
+    padded = round_up(half_cells + 2 * SIDE, TILE)
     pose_total = lax.axis_size("pose") // XPLANES
     vmem = pl.BlockSpec(memory_space=pltpu.VMEM)
-    hbm = pl.BlockSpec(memory_space=pl.ANY)
     return pl.pallas_call(
         functools.partial(main_kernel, chunk, pose_total, XPLANES),
-        out_shape=jax.ShapeDtypeStruct((copies, LANES), f32),
-        in_specs=[vmem] * 3 + [hbm] * 2 + [vmem] * 3 + [hbm, vmem],
+        out_shape=pltpu.VMEM((copies, LANES), f32),
+        in_specs=[vmem] * 9,
         out_specs=vmem,
         scratch_shapes=[
             pltpu.VMEM((8, plane_cells + 3 * LANES), jnp.int32),
             pltpu.VMEM((5, padded, depth), bf16),
-            pltpu.VMEM((5, padded, rest.shape[1]), fp8),
             pltpu.VMEM((3, padded, mid), bf16),
             pltpu.VMEM((9, padded + 16, width), f32),
-            pltpu.VMEM(weight2.shape, bf16),
             pltpu.VMEM((width, half_cells), f32),
-            pltpu.SemaphoreType.DMA((3,)),
         ],
+        compiler_params=pltpu.CompilerParams(vmem_limit_bytes=40 << 20),
         name="rescore",
-    )(own, near, far, head_own, head_far, folded, rest, bias1, weight2, bias2)
+    )(
+        in_vmem(own),
+        in_vmem(near),
+        in_vmem(far),
+        in_vmem(head_own),
+        in_vmem(head_far),
+        in_vmem(folded),
+        bias1,
+        in_vmem(weight2),
+        bias2,
+    )
 
 
 def final_kernel(pose_total, chan_count, parts_ref, plane_ref, scores_ref):
@@ -288,8 +278,9 @@
             jax.ShapeDtypeStruct((pose_total,), f32),
         ),
         out_specs=(smem, smem),
+        compiler_params=pltpu.CompilerParams(vmem_limit_bytes=1 << 20),
         name="final_sums",
-    )(parts)
+    )(in_vmem(parts))
 
 
 def on_device(
@@ -317,8 +308,10 @@
         return lax.ppermute(code, ("pose", "chan"), pairs)
 
     code = atom_type * 4 + occupancy
-    near = jnp.concatenate([fetch(1), fetch(2)], axis=1)
-    folded, rest = fold_embedding(atom_embed, conv1_weight)
+    first, second, folded = lax.optimization_barrier(
+        (fetch(1), fetch(2), fold_embedding(atom_embed, conv1_weight))
+    )
+    near = jnp.concatenate([first, second], axis=1)
     far = lax.ppermute(near, "chan", swap)
     head_far = lax.ppermute(head_weight, "chan", swap)
     part = rescore(
@@ -328,7 +321,6 @@
         head_weight,
         head_far,
         folded,
-        rest,
         conv1_bias[None, :],
         conv2_weight,
         conv2_bias[None, :],

time: 36.2 us -> 31.6 us (0.87)
  Pallas kernels: 14.4 us -> 9.65 us
  local copies, waits for them, and re-layouts: 0.81 us -> 2.2 us
  waiting for transfers between devices: 2.31 us -> 1.18 us
    pallas_call x1, Pallas kernels: 2.92 us -> 0.47 us  [fold_embedding(): pl.pallas_call(fold_kernel, out_shape=pltpu.VMEM((3, depth, mid), bf16),...]
    ppermute x2, waiting for transfers between devices: 2.3 us -> 0.01 us  [fetch(): return lax.ppermute(code, ('pose', 'chan'), pairs)]
    pallas_call x1, Pallas kernels: 10.1 us -> 8.53 us  [rescore(): pl.pallas_call(functools.partial(main_kernel, chunk, pose_total, XPLANES)...]
    unnamed x9 -> x13, local copies, waits for them, and re-layouts: 0.81 us -> 2.19 us
    ppermute x1, waiting for transfers between devices: 0.01 us -> 1.17 us  [on_device(): far = lax.ppermute(near, 'chan', swap)]
    pallas_call x1, Pallas kernels: 1.38 us -> 0.66 us  [final_sums(): pl.pallas_call(functools.partial(final_kernel, pose_total, chan_count), o...]
  transfers between devices with their start and end apart: 4 -> 4, of which waited for: 2 -> 1; matrix products, arithmetic and copies ran while one was open for 0% -> 0% of each run, Pallas kernels for 8% -> 1%
where the time goes in v2:
time: 31.6 us; the launch traced here: 31.3 us
  blocking collectives  12.8 us (41%)
  Pallas kernels  9.65 us (31%)
  starting transfers between devices  3.89 us (12%)
  local copies, waits for them, and re-layouts  2.2 us (7%)
  waiting for transfers between devices  1.18 us (4%)
  other arithmetic  0.86 us (3%)
  between operations  0.72 us (2%)
    all_to_all x1, blocking collectives, on_device(): parts = lax.all_to_all(part[:, None, :], ('pose', 'chan'), 0, 0, tiled=True)  12.8 us
    pallas_call x1, Pallas kernels, rescore(): pl.pallas_call(functools.partial(main_kernel, chunk, pose_total, XPLANES)...  8.53 us
    ppermute x2, starting transfers between devices, fetch(): return lax.ppermute(code, ('pose', 'chan'), pairs)  2.61 us
    unnamed x13, local copies, waits for them, and re-layouts  2.19 us
    ppermute x1, starting transfers between devices, on_device(): head_far = lax.ppermute(head_weight, 'chan', swap)  1.21 us
    ppermute x1, waiting for transfers between devices, on_device(): far = lax.ppermute(near, 'chan', swap)  1.17 us
    add x1, other arithmetic, on_device(): code = atom_type * 4 + occupancy  0.86 us
    pallas_call x1, Pallas kernels, final_sums(): pl.pallas_call(functools.partial(final_kernel, pose_total, chan_count), o...  0.66 us
  transfers between devices with their start and end apart: 4, of which 1 were waited for; matrix products, arithmetic and copies ran while one was open for 0% of the time, Pallas kernels for 1%

profile of v2, /device:TPU:0, one launch (start us, length us, event | category | flops | bytes accessed | tf_op | source)
XLA Modules:
  0.0 31.3 jit_solution(15781802765638932759)
XLA Ops:
  0.6 0.0 copy-start
  0.6 0.9 %multiply_add_fusion.own_ref = s32[1,2304]{1,0:T(1,128)S(1)} fusion(s32[1,2304]{1,0:T(1,128)} %param.9, s32[1,2304]{1,0:T(1,128)} %param.8), kind=kLoop, calls=%fused_computation | loop fusion | flops 4608 | bytes 27648 | tf_op jit(solution)/shard_map/add | solution.py:310
  1.5 0.5 %collective-permute-start.1 = (s32[1,2304]{1,0:T(1,128)S(1)}, s32[1,2304]{1,0:T(1,128)S(1)}, u32[]{:S(2)}, u32[]{:S(2)}) collective-permute-start(s32[1,2304]{1,0:T(1,128)S(1)} %multiply_add_fusion.own_ref), channel_id=1, source_target_pairs={{0,1},{1,5},{2,3},{3,7},{4,0},{5,9},{6,2},{7,11},{8,4},{9,13},{10,... | collective-permute-start | bytes 27656 | tf_op jit(solution)/shard_map/ppermute | solution.py:308
  2.1 2.1 %collective-permute-start = (s32[1,2304]{1,0:T(1,128)S(1)}, s32[1,2304]{1,0:T(1,128)S(1)}, u32[]{:S(2)}, u32[]{:S(2)}) collective-permute-start(s32[1,2304]{1,0:T(1,128)S(1)} %multiply_add_fusion.own_ref), channel_id=1, source_target_pairs={{0,1},{1,3},{2,0},{3,5},{4,2},{5,7},{6,4},{7,9},{8,6},{9,11},{10,8... | collective-permute-start | bytes 27656 | tf_op jit(solution)/shard_map/ppermute | solution.py:308
  4.1 1.2 %collective-permute-start.3 = (f32[64,2304]{1,0:T(8,128)}, f32[64,2304]{1,0:T(8,128)S(1)}, u32[]{:S(2)}, u32[]{:S(2)}) collective-permute-start(f32[64,2304]{1,0:T(8,128)} %head_own_ref.1), channel_id=1, source_target_pairs={{0,1},{1,0},{2,3},{3,2},{4,5},{5,4},{6,7},{7,6},{8,9},{9,8},{10,11... | collective-permute-start | bytes 1769480 | tf_op jit(solution)/shard_map/ppermute | solution.py:316
  5.3 0.0 copy-start.1
  5.3 1.5 %copy-done.1 = bf16[27,128,256]{2,1,0:T(8,128)(2,1)S(1)} copy-done((bf16[27,128,256]{2,1,0:T(8,128)(2,1)S(1)}, bf16[27,128,256]{2,1,0:T(8,128)(2,1)}, u32[]{:S(2)}) %copy-start.1) | copy-done | bytes 1769496
  6.8 0.0 copy-start.3
  6.8 0.7 %copy-done.3 = bf16[28,128]{1,0:T(8,128)(2,1)S(1)} copy-done((bf16[28,128]{1,0:T(8,128)(2,1)S(1)}, bf16[28,128]{1,0:T(8,128)(2,1)}, u32[]{:S(2)}) %copy-start.3) | copy-done | bytes 7192
  7.5 0.0 copy-start.2
  7.5 0.0 copy-start.4
  7.5 0.0 copy-start.5
  7.5 0.5 %fold_embedding.1.folded_ref = bf16[3,768,256]{2,1,0:T(8,128)(2,1)S(1)} custom-call(bf16[28,128]{1,0:T(8,128)(2,1)S(1)} %copy-done.3, bf16[27,128,256]{2,1,0:T(8,128)(2,1)S(1)} %copy-done.1), custom_call_target="tpu_custom_call" | custom-call | tf_op jit(solution)/shard_map/fold_embedding/pallas_call | solution.py:51
  8.0 0.0 collective-permute-done.1
  8.0 0.0 collective-permute-done
  8.0 0.1 collective-permute-start.2
  8.1 1.2 %collective-permute-done.2.far_ref = s32[1,4608]{1,0:T(1,128)S(1)} collective-permute-done((s32[1,4608]{1,0:T(1,128)S(1)}, s32[1,4608]{1,0:T(1,128)S(1)}, u32[]{:S(2)}, u32[]{:S(2)}) %collective-permute-start.2) | collective-permute-done | bytes 18464 | tf_op jit(solution)/shard_map/ppermute | solution.py:315
  9.3 0.0 collective-permute-done.3.head_far_ref
  9.3 0.0 copy-done
  9.3 0.0 copy-done.2
  9.3 0.0 copy-done.4
  9.3 0.0 copy-done.5
  9.3 8.5 %rescore.1 = f32[32,128]{1,0:T(8,128)S(1)} custom-call(s32[1,2304]{1,0:T(1,128)S(1)} %multiply_add_fusion.own_ref, s32[1,4608]{1,0:T(1,128)S(1)} %constant_dynamic-update-slice_fusion.near_ref, s32[1,4608]{1,0:T(1,128)S(1)} %collective-permute-done.2.far_ref, f32[64,2304]{1,0:T(8,128)S(1)} %copy-done.2, f32[64,2304]{1,0:T(8,128)S(1)} %collective-permute-done.3.head_far_ref, ...), custom_call_target="tpu_custom_call" | custom-call | tf_op jit(solution)/shard_map/rescore/pallas_call | solution.py:236
  17.8 12.8 %all_to_all.5.parts_ref = f32[32,1,128]{2,1,0:T(1,128)S(1)} all-to-all(f32[32,1,128]{2,1,0:T(1,128)S(1)} %bitcast.3), channel_id=1, replica_groups=mesh['pose'=16,'chan'=2] {'pose','chan'}, dimensions={0} | all-to-all | bytes 32768 | tf_op jit(solution)/shard_map/all_to_all | solution.py:329
  30.7 0.7 %final_sums.1 = (f32[1]{0:T(128)}, f32[1]{0:T(128)}) custom-call(f32[32,1,128]{2,1,0:T(1,128)S(1)} %all_to_all.5.parts_ref), custom_call_target="tpu_custom_call" | custom-call | tf_op jit(solution)/shard_map/final_sums/pallas_call | solution.py:274
  (2 shorter events, 0.0 us)
Async XLA Ops:
  0.6 8.6 %copy-start = (bf16[27,256,128]{2,1,0:T(8,128)(2,1)S(1)}, bf16[27,256,128]{2,1,0:T(8,128)(2,1)}, u32[]{:S(2)}) copy-start(bf16[27,256,128]{2,1,0:T(8,128)(2,1)} %weight2_ref.1) | copy-start | bytes 5308420
  1.5 6.5 %collective-permute-start.1 = (s32[1,2304]{1,0:T(1,128)S(1)}, s32[1,2304]{1,0:T(1,128)S(1)}, u32[]{:S(2)}, u32[]{:S(2)}) collective-permute-start(s32[1,2304]{1,0:T(1,128)S(1)} %multiply_add_fusion.own_ref), channel_id=1, source_target_pairs={{0,1},{1,5},{2,3},{3,7},{4,0},{5,9},{6,2},{7,11},{8,4},{9,13},{10,... | collective-permute-start | bytes 27656 | tf_op jit(solution)/shard_map/ppermute | solution.py:308
  2.1 5.9 %collective-permute-start = (s32[1,2304]{1,0:T(1,128)S(1)}, s32[1,2304]{1,0:T(1,128)S(1)}, u32[]{:S(2)}, u32[]{:S(2)}) collective-permute-start(s32[1,2304]{1,0:T(1,128)S(1)} %multiply_add_fusion.own_ref), channel_id=1, source_target_pairs={{0,1},{1,3},{2,0},{3,5},{4,2},{5,7},{6,4},{7,9},{8,6},{9,11},{10,8... | collective-permute-start | bytes 27656 | tf_op jit(solution)/shard_map/ppermute | solution.py:308
  4.1 5.2 %collective-permute-start.3 = (f32[64,2304]{1,0:T(8,128)}, f32[64,2304]{1,0:T(8,128)S(1)}, u32[]{:S(2)}, u32[]{:S(2)}) collective-permute-start(f32[64,2304]{1,0:T(8,128)} %head_own_ref.1), channel_id=1, source_target_pairs={{0,1},{1,0},{2,3},{3,2},{4,5},{5,4},{6,7},{7,6},{8,9},{9,8},{10,11... | collective-permute-start | bytes 1769480 | tf_op jit(solution)/shard_map/ppermute | solution.py:316
  5.3 1.5 %copy-start.1 = (bf16[27,128,256]{2,1,0:T(8,128)(2,1)S(1)}, bf16[27,128,256]{2,1,0:T(8,128)(2,1)}, u32[]{:S(2)}) copy-start(bf16[27,128,256]{2,1,0:T(8,128)(2,1)} %weight_ref.1) | copy-start | bytes 5308420
  6.8 0.7 %copy-start.3 = (bf16[28,128]{1,0:T(8,128)(2,1)S(1)}, bf16[28,128]{1,0:T(8,128)(2,1)}, u32[]{:S(2)}) copy-start(bf16[28,128]{1,0:T(8,128)(2,1)} %embed_ref.1) | copy-start | bytes 21508
  7.5 1.8 %copy-start.2 = (f32[64,2304]{1,0:T(8,128)S(1)}, f32[64,2304]{1,0:T(8,128)}, u32[]{:S(2)}) copy-start(f32[64,2304]{1,0:T(8,128)} %head_own_ref.1) | copy-start | bytes 1769476
  7.5 1.8 %copy-start.4 = (f32[256]{0:T(256)S(1)}, f32[256]{0:T(256)}, u32[]{:S(2)}) copy-start(f32[256]{0:T(256)} %param.12) | copy-start | bytes 3076
  7.5 1.8 %copy-start.5 = (f32[128]{0:T(128)S(1)}, f32[128]{0:T(128)}, u32[]{:S(2)}) copy-start(f32[128]{0:T(128)} %param.14) | copy-start | bytes 1540
  8.0 1.3 %collective-permute-start.2 = (s32[1,4608]{1,0:T(1,128)S(1)}, s32[1,4608]{1,0:T(1,128)S(1)}, u32[]{:S(2)}, u32[]{:S(2)}) collective-permute-start(s32[1,4608]{1,0:T(1,128)S(1)} %constant_dynamic-update-slice_fusion.near_ref), channel_id=1, source_target_pairs={{0,1},{1,0},{2,3},{3,2},{4,5},{5,4},{6,7},{7,6},{8,9},{9,8},{10,11... | collective-permute-start | bytes 55304 | tf_op jit(solution)/shard_map/ppermute | solution.py:315

commit v3 on v2

v3 whole, which is shorter than its diff:
```python
import functools

import jax
import jax.numpy as jnp
from jax import lax
from jax.experimental import pallas as pl
from jax.experimental.pallas import tpu as pltpu
from jax.sharding import PartitionSpec as P

SIDE = 48
XPLANES = 16
LANES = 128
TILE = 256
PARTS = 3
TAPS = [(shift_y, shift_z) for shift_y in (-1, 0, 1) for shift_z in (-1, 0, 1)]

bf16 = jnp.bfloat16
f32 = jnp.float32


def in_vmem(array):
    return pltpu.with_memory_space_constraint(array, pltpu.VMEM)


def in_hbm(array):
    return pltpu.with_memory_space_constraint(array, pltpu.HBM)


def round_up(value, step):
    return -(-value // step) * step


def params(megabytes):
    return pltpu.CompilerParams(vmem_limit_bytes=megabytes << 20)


def encode_kernel(type_hbm, count_hbm, embed_hbm, code_ref, pair_ref, type_ref, count_ref, embed_ref, sems):
    types = embed_ref.shape[0]
    half = pair_ref.shape[0] // 2
    copies = [
        pltpu.make_async_copy(source, target, sems.at[n])
        for n, (source, target) in enumerate(
            ((type_hbm, type_ref), (count_hbm, count_ref), (embed_hbm, embed_ref))
        )
    ]
    for copy in copies:
        copy.start()
    pair_ref[...] = jnp.zeros_like(pair_ref)
    for copy in copies:
        copy.wait()
    code_ref[...] = type_ref[...] * 4 + count_ref[...]
    embed = embed_ref[...].astype(f32)
    pair_ref[:types, :] = embed
    pair_ref[half:half + types, :] = (3.0 * embed).astype(bf16).astype(f32)


def encode(atom_type, occupancy, atom_embed):
    types, width = atom_embed.shape
    return pl.pallas_call(
        encode_kernel,
        out_shape=(
            pltpu.VMEM(atom_type.shape, jnp.int32),
            pltpu.VMEM((2 * round_up(types, 16), width), f32),
        ),
        in_specs=[pl.BlockSpec(memory_space=pl.ANY)] * 3,
        scratch_shapes=[
            pltpu.VMEM(atom_type.shape, jnp.int32),
            pltpu.VMEM(atom_type.shape, jnp.int32),
            pltpu.VMEM(atom_embed.shape, bf16),
            pltpu.SemaphoreType.DMA((3,)),
        ],
        compiler_params=params(1),
        name="encode",
    )(in_hbm(atom_type), in_hbm(occupancy), in_hbm(atom_embed))


def fold_kernel(types, pair_ref, weight_ref, folded_ref, rows_ref):
    half = pair_ref.shape[0] // 2
    rest = round_up(9 * types, LANES)
    pair = pair_ref[...].astype(bf16)
    rows_ref[...] = jnp.zeros_like(rows_ref)
    for dx in range(3):
        for tap in range(9):
            both = jnp.dot(pair, weight_ref[dx * 9 + tap], preferred_element_type=f32)
            once, thrice = both[:types, :], both[half:half + types, :]
            rounded = once.astype(bf16).astype(f32)
            first = rest + 2 * types * tap
            rows_ref[dx, types * tap:types * (tap + 1), :] = rounded
            rows_ref[dx, first:first + types, :] = once - rounded
            rows_ref[dx, first + types:first + 2 * types, :] = thrice - 3.0 * rounded
        folded_ref[dx] = rows_ref[dx].astype(bf16)


def fold_embedding(types, pair, conv1_weight):
    mid = conv1_weight.shape[2]
    depth = round_up(9 * types, LANES) + round_up(18 * types, LANES)
    return pl.pallas_call(
        functools.partial(fold_kernel, types),
        out_shape=pltpu.VMEM((3, depth, mid), bf16),
        scratch_shapes=[pltpu.VMEM((3, depth, mid), f32)],
        compiler_params=params(12),
        name="fold_embedding",
    )(in_vmem(pair), in_vmem(conv1_weight))


def one_hot(rows, x, types, start):
    width = TILE
    depth = round_up(types * len(rows), LANES)
    sub = lax.broadcasted_iota(jnp.int32, (8, 1), 0)

    def spread(row):
        return jnp.broadcast_to(row[x:x + 1, start:start + width], (8, width))

    groups = []
    for first in range(0, depth, 8):
        low, high = first // types, (first + 7) // types
        if low >= len(rows):
            groups.append(jnp.zeros((8, width), f32))
            continue
        kind, count = spread(rows[low][0]), spread(rows[low][1])
        number = sub + (first - types * low)
        if high != low:
            own = sub < types * high - first
            number = jnp.where(own, number, number - types)
            if high < len(rows):
                kind = jnp.where(own, kind, spread(rows[high][0]))
                count = jnp.where(own, count, spread(rows[high][1]))
            else:
                count = jnp.where(own, count, 0.0)
        groups.append(jnp.where(kind == number, count, 0.0))
    return jnp.concatenate(groups, axis=0)


def position(pose_total):
    chan = lax.axis_index("chan")
    block = lax.axis_index("pose") // pose_total
    behind = jnp.where(chan == 1, block, XPLANES - 1 - block)
    return chan, behind, [jnp.where(chan == 1, dx, 2 - dx) for dx in range(3)]


def tap_rows(planes_ref, rows, chan, padded, types):
    plane_cells = rows[0].shape[1]
    half_cells = plane_cells // 2
    planes_ref[...] = jnp.zeros_like(planes_ref)
    for x, row in enumerate(rows):
        planes_ref[x:x + 1, LANES:LANES + plane_cells] = row
    start = pl.multiple_of(chan * half_cells, LANES)
    cells = planes_ref[:, pl.ds(start, half_cells + 3 * LANES)]
    column = lax.rem(lax.broadcasted_iota(jnp.int32, (8, padded), 1), SIDE)
    plain, split = [], []
    for shift_y, shift_z in TAPS:
        first = LANES - SIDE + SIDE * shift_y + shift_z
        moved = cells[:, first:first + padded]
        inside = (column + shift_z >= 0) & (column + shift_z < SIDE)
        moved = jnp.where(inside, moved, 0)
        kind = lax.shift_right_logical(moved, 2)
        count = moved & 3
        plain.append((kind, count.astype(f32)))
        split.append(
            (
                jnp.where(count == 3, kind + types, kind),
                jnp.where(count == 3, 1, count).astype(f32),
            )
        )
    return plain, split


def both_hot(plain, split, x, types, first):
    return jnp.concatenate(
        [one_hot(plain, x, types, first), one_hot(split, x, 2 * types, first)], axis=0
    ).astype(bf16).T


def hidden_rows(operands, bias1, folded_ref, order, first, size, half_cells, chan, plane_ok):
    total = bias1
    for dx in range(3):
        total = total + jnp.dot(
            operands[dx](first, size), folded_ref[order[dx]], preferred_element_type=f32
        )
    index = first + lax.broadcasted_iota(jnp.int32, (size, 1), 0)
    lowest = jnp.where(plane_ok, jnp.where(chan == 0, SIDE, 0), half_cells + 2 * SIDE)
    highest = jnp.where(chan == 0, half_cells + 2 * SIDE, half_cells + SIDE)
    inside = (index >= lowest) & (index < highest)
    return jnp.where(inside, jnp.maximum(total, 0.0), 0.0).astype(bf16)


def reader(ref, x):
    return lambda first, size: ref[x, first:first + size, :]


def score_kernel(
    pose_total,
    types,
    own_ref,
    near_ref,
    far_ref,
    head_own_ref,
    head_far_ref,
    folded_ref,
    bias1_ref,
    weight2_ref,
    bias2_ref,
    out_ref,
    planes_ref,
    hot_ref,
    hidden_ref,
    sums_ref,
    head_ref,
):
    chan, behind, order = position(pose_total)
    plane_cells = own_ref.shape[1]
    half_cells = plane_cells // 2
    padded = hot_ref.shape[1]
    used = half_cells + 2 * SIDE
    share = head_own_ref.shape[0]
    head_cells = pl.ds(pl.multiple_of(chan * half_cells, LANES), half_cells)
    head_ref[pl.ds(pl.multiple_of(chan * share, share), share), :] = head_own_ref[:, head_cells]
    head_ref[pl.ds(pl.multiple_of((1 - chan) * share, share), share), :] = head_far_ref[
        :, head_cells
    ]
    near, far = near_ref[...], far_ref[...]
    rows = [
        jnp.where(behind >= 2, near[:, plane_cells:], 0),
        jnp.where(behind >= 1, near[:, :plane_cells], 0),
        own_ref[...],
        jnp.where(behind <= XPLANES - 2, far[:, :plane_cells], 0),
        jnp.where(behind <= XPLANES - 3, far[:, plane_cells:], 0),
    ]
    plain, split = tap_rows(planes_ref, rows, chan, padded, types)
    bias1 = bias1_ref[...]
    operands = [reader(hot_ref, x) for x in range(5)]
    plane_ok = [behind >= 1, True, behind <= XPLANES - 2]
    for first in range(0, padded, TILE):
        size = min(TILE, used - first)
        for x in range(5):
            hot_ref[x, first:first + TILE, :] = both_hot(plain, split, x, types, first)
            if x >= 2:
                h = x - 2
                hidden_ref[h, first:first + size, :] = hidden_rows(
                    operands[h:], bias1, folded_ref, order, first, size, half_cells, chan, plane_ok[h]
                )

    width = weight2_ref.shape[2]
    hidden = [reader(hidden_ref, h) for h in range(3)]

    def taps(first, size, *numbers):
        total = None
        for h in range(3):
            weights = [weight2_ref[order[h] * 9 + tap] for tap in numbers]
            part = jnp.dot(
                hidden[h](first, size),
                jnp.concatenate(weights, axis=1),
                preferred_element_type=f32,
            )
            total = part if total is None else total + part
        return [total[:, n * width:(n + 1) * width] for n in range(len(numbers))]

    ends = [(0, half_cells), (0, half_cells + SIDE), (SIDE, half_cells + SIDE), (2 * SIDE, used), (2 * SIDE, used)]
    for pair, (begin, end) in enumerate(ends):
        size = (end - begin) // PARTS
        numbers = [2 * pair, 2 * pair + 1][: 2 if pair < 4 else 1]
        for first in range(begin, end, size):
            for number, value in zip(numbers, taps(first, size, *numbers)):
                sums_ref[number, 8 + first:8 + first + size, :] = value
    bias2 = bias2_ref[...]
    running = jnp.zeros((8, width), f32)
    for first in range(0, half_cells, LANES):
        moved = []
        for shift_z in range(3):
            offset = 8 + first + shift_z - 1
            moved.append(
                sums_ref[shift_z, offset:offset + LANES, :]
                + sums_ref[3 + shift_z, offset + SIDE:offset + SIDE + LANES, :]
                + sums_ref[6 + shift_z, offset + 2 * SIDE:offset + 2 * SIDE + LANES, :]
            )
        column = lax.rem(first + lax.broadcasted_iota(jnp.int32, (LANES, 1), 0), SIDE)
        mapped = (
            bias2
            + moved[1]
            + jnp.where(column > 0, moved[0], 0.0)
            + jnp.where(column < SIDE - 1, moved[2], 0.0)
        )
        scored = jnp.maximum(mapped, 0.0) * head_ref[:, first:first + LANES].T
        running = running + jnp.sum(scored.reshape(LANES // 8, 8, width), axis=0)
    out_ref[...] = jnp.broadcast_to(jnp.sum(running), out_ref.shape)


def score(types, pose_total, own, near, far, head_own, head_far, folded, bias1, weight2, bias2, copies):
    plane_cells = own.shape[1]
    depth, mid = folded.shape[1:]
    width = weight2.shape[2]
    padded = round_up(plane_cells // 2 + 2 * SIDE, TILE)
    return pl.pallas_call(
        functools.partial(score_kernel, pose_total, types),
        out_shape=pltpu.VMEM((copies, LANES), f32),
        scratch_shapes=[
            pltpu.VMEM((8, plane_cells + 3 * LANES), jnp.int32),
            pltpu.VMEM((5, padded, depth), bf16),
            pltpu.VMEM((3, padded, mid), bf16),
            pltpu.VMEM((9, padded + 16, width), f32),
            pltpu.VMEM((width, plane_cells // 2), f32),
        ],
        compiler_params=params(40),
        name="score",
    )(
        in_vmem(own),
        in_vmem(near),
        in_vmem(far),
        in_vmem(head_own),
        in_vmem(head_far),
        in_vmem(folded),
        in_vmem(bias1),
        in_vmem(weight2),
        in_vmem(bias2),
    )


def final_kernel(pose_total, chan_count, parts_ref, plane_ref, scores_ref):
    parts = parts_ref[:, 0, :]
    pose = lax.broadcasted_iota(jnp.int32, parts.shape, 0) // chan_count
    first = lax.broadcasted_iota(jnp.int32, parts.shape, 1) == 0
    plane_ref[0] = jnp.sum(jnp.where(first & (pose == lax.axis_index("pose")), parts, 0.0))
    for p in range(pose_total):
        scores_ref[p] = jnp.sum(jnp.where(first & (lax.rem(pose, pose_total) == p), parts, 0.0))


def final_sums(parts, pose_total, chan_count):
    smem = pl.BlockSpec(memory_space=pltpu.SMEM)
    return pl.pallas_call(
        functools.partial(final_kernel, pose_total, chan_count),
        out_shape=(
            jax.ShapeDtypeStruct((1,), f32),
            jax.ShapeDtypeStruct((pose_total,), f32),
        ),
        out_specs=(smem, smem),
        compiler_params=params(1),
        name="final_sums",
    )(in_vmem(parts))


def on_device(
    atom_type,
    occupancy,
    atom_embed,
    conv1_weight,
    conv1_bias,
    conv2_weight,
    conv2_bias,
    head_weight,
):
    chan_count = lax.axis_size("chan")
    pose_count = lax.axis_size("pose")
    pose_total = pose_count // XPLANES
    swap = [(0, 1), (1, 0)]

    def fetch(steps):
        by = steps * pose_total
        pairs = []
        for i in range(pose_count):
            up = 2 * (i + by) + 1 if i + by < pose_count else 2 * i
            down = 2 * (i - by) if i >= by else 2 * i + 1
            pairs += [(2 * i, down), (2 * i + 1, up)]
        return lax.ppermute(code, ("pose", "chan"), pairs)

    types = atom_embed.shape[0]
    code, pair = encode(atom_type, occupancy, atom_embed)
    second, first, folded = lax.optimization_barrier(
        (fetch(2), fetch(1), fold_embedding(types, pair, conv1_weight))
    )
    near = jnp.concatenate([first, second], axis=1)
    far = lax.ppermute(near, "chan", swap)
    head_far = lax.ppermute(head_weight, "chan", swap)
    part = score(
        types,
        pose_total,
        code,
        near,
        far,
        head_weight,
        head_far,
        folded,
        conv1_bias[None, :],
        conv2_weight,
        conv2_bias[None, :],
        pose_count * chan_count,
    )
    parts = lax.all_to_all(part[:, None, :], ("pose", "chan"), 0, 0, tiled=True)
    return final_sums(parts, pose_total, chan_count)


def solution(mesh):
    return jax.shard_map(
        on_device,
        mesh=mesh,
        in_specs=(P("pose", None), P("pose", None), P(), P(), P(), P(), P(), P("chan", None)),
        out_specs=(P("pose"), P()),
        check_vma=False,
    )
```

time: 31.6 us -> 30.9 us (0.978)
  other arithmetic: 0.86 us -> 0 us
  local copies, waits for them, and re-layouts: 2.2 us -> 1.5 us
  Pallas kernels: 9.65 us -> 10.3 us
  waiting for transfers between devices: 1.18 us -> 1.54 us
    add x1 -> x0, other arithmetic: 0.86 us -> none  [on_device(): code = atom_type * 4 + occupancy]
    unnamed x13 -> x11, local copies, waits for them, and re-layouts: 2.19 us -> 1.49 us
    pallas_call x2 -> x3, Pallas kernels: 8.99 us -> 9.64 us  [the longest x1 8.3 us: score(): pl.pallas_call(functools.partial(score_kernel, pose_total, types), out_sh...]
    ppermute x2, waiting for transfers between devices: 0.01 us -> 0.35 us  [fetch(): return lax.ppermute(code, ('pose', 'chan'), pairs)]
  transfers between devices with their start and end apart: 4 -> 4, of which waited for: 1 -> 2; matrix products, arithmetic and copies ran while one was open for 0% -> 0% of each run, Pallas kernels for 1% -> 1%
where the time goes in v3:
time: 30.9 us; the launch traced here: 30.6 us
  blocking collectives  12.8 us (41%)
  Pallas kernels  10.3 us (33%)
  starting transfers between devices  3.82 us (12%)
  waiting for transfers between devices  1.54 us (5%)
  local copies, waits for them, and re-layouts  1.5 us (5%)
  between operations  0.7 us (2%)
    all_to_all x1, blocking collectives, on_device(): parts = lax.all_to_all(part[:, None, :], ('pose', 'chan'), 0, 0, tiled=True)  12.8 us
    pallas_call x1, Pallas kernels, score(): pl.pallas_call(functools.partial(score_kernel, pose_total, types), out_sh...  8.3 us
    ppermute x2, starting transfers between devices, fetch(): return lax.ppermute(code, ('pose', 'chan'), pairs)  2.58 us
    unnamed x11, local copies, waits for them, and re-layouts  1.49 us
    ppermute x1, starting transfers between devices, on_device(): head_far = lax.ppermute(head_weight, 'chan', swap)  1.24 us
    ppermute x1, waiting for transfers between devices, on_device(): far = lax.ppermute(near, 'chan', swap)  1.18 us
    pallas_call x1, Pallas kernels, encode(): pl.pallas_call(encode_kernel, out_shape=(pltpu.VMEM(atom_type.shape, jnp....  0.89 us
    pallas_call x1, Pallas kernels, final_sums(): pl.pallas_call(functools.partial(final_kernel, pose_total, chan_count), o...  0.66 us
  transfers between devices with their start and end apart: 4, of which 2 were waited for; matrix products, arithmetic and copies ran while one was open for 0% of the time, Pallas kernels for 1%

profile of v3, /device:TPU:0, one launch (start us, length us, event | category | flops | bytes accessed | tf_op | source)
XLA Modules:
  0.0 30.6 jit_solution(17280991357675304838)
XLA Ops:
  0.6 0.0 copy-start
  0.6 0.9 %encode.1 = (s32[1,2304]{1,0:T(1,128)S(1)}, f32[64,128]{1,0:T(8,128)S(1)}) custom-call(s32[1,2304]{1,0:T(1,128)} %type_hbm.1, s32[1,2304]{1,0:T(1,128)} %count_hbm.1, bf16[28,128]{1,0:T(8,128)(2,1)} %embed_hbm.1), custom_call_target="tpu_custom_call" | custom-call | tf_op jit(solution)/shard_map/encode/pallas_call | solution.py:59
  1.5 0.5 %collective-permute-start.1 = (s32[1,2304]{1,0:T(1,128)S(1)}, s32[1,2304]{1,0:T(1,128)S(1)}, u32[]{:S(2)}, u32[]{:S(2)}) collective-permute-start(s32[1,2304]{1,0:T(1,128)S(1)} %get-tuple-element.7.own_ref), channel_id=1, source_target_pairs={{0,1},{1,3},{2,0},{3,5},{4,2},{5,7},{6,4},{7,9},{8,6},{9,11},{10,8... | collective-permute-start | bytes 27656 | tf_op jit(solution)/shard_map/ppermute | solution.py:363
  2.1 2.0 %collective-permute-start = (s32[1,2304]{1,0:T(1,128)S(1)}, s32[1,2304]{1,0:T(1,128)S(1)}, u32[]{:S(2)}, u32[]{:S(2)}) collective-permute-start(s32[1,2304]{1,0:T(1,128)S(1)} %get-tuple-element.7.own_ref), channel_id=1, source_target_pairs={{0,1},{1,5},{2,3},{3,7},{4,0},{5,9},{6,2},{7,11},{8,4},{9,13},{10,... | collective-permute-start | bytes 27656 | tf_op jit(solution)/shard_map/ppermute | solution.py:363
  4.1 1.2 %collective-permute-start.3 = (f32[64,2304]{1,0:T(8,128)}, f32[64,2304]{1,0:T(8,128)S(1)}, u32[]{:S(2)}, u32[]{:S(2)}) collective-permute-start(f32[64,2304]{1,0:T(8,128)} %head_own_ref.1), channel_id=1, source_target_pairs={{0,1},{1,0},{2,3},{3,2},{4,5},{5,4},{6,7},{7,6},{8,9},{9,8},{10,11... | collective-permute-start | bytes 1769480 | tf_op jit(solution)/shard_map/ppermute | solution.py:372
  5.4 0.0 copy-start.1
  5.4 1.5 %copy-done.1 = bf16[27,128,256]{2,1,0:T(8,128)(2,1)S(1)} copy-done((bf16[27,128,256]{2,1,0:T(8,128)(2,1)S(1)}, bf16[27,128,256]{2,1,0:T(8,128)(2,1)}, u32[]{:S(2)}) %copy-start.1) | copy-done | bytes 1769496
  6.8 0.0 copy-start.2
  6.8 0.0 copy-start.3
  6.8 0.0 copy-start.4
  6.8 0.5 %fold_embedding.1.folded_ref = bf16[3,768,256]{2,1,0:T(8,128)(2,1)S(1)} custom-call(f32[64,128]{1,0:T(8,128)S(1)} %get-tuple-element.8.pair_ref, bf16[27,128,256]{2,1,0:T(8,128)(2,1)S(1)} %copy-done.1), custom_call_target="tpu_custom_call" | custom-call | tf_op jit(solution)/shard_map/fold_embedding/pallas_call | solution.py:97
  7.3 0.0 collective-permute-done.1
  7.3 0.4 %collective-permute-done = s32[1,2304]{1,0:T(1,128)S(1)} collective-permute-done((s32[1,2304]{1,0:T(1,128)S(1)}, s32[1,2304]{1,0:T(1,128)S(1)}, u32[]{:S(2)}, u32[]{:S(2)}) %collective-permute-start) | collective-permute-done | bytes 9248 | tf_op jit(solution)/shard_map/ppermute | solution.py:363
  7.7 0.0 collective-permute-start.2
  7.7 1.2 %collective-permute-done.2.far_ref = s32[1,4608]{1,0:T(1,128)S(1)} collective-permute-done((s32[1,4608]{1,0:T(1,128)S(1)}, s32[1,4608]{1,0:T(1,128)S(1)}, u32[]{:S(2)}, u32[]{:S(2)}) %collective-permute-start.2) | collective-permute-done | bytes 18464 | tf_op jit(solution)/shard_map/ppermute | solution.py:371
  8.9 0.0 collective-permute-done.3.head_far_ref
  8.9 0.0 copy-done
  8.9 0.0 copy-done.2
  8.9 0.0 copy-done.3
  8.9 0.0 copy-done.4
  8.9 8.3 %score.1 = f32[32,128]{1,0:T(8,128)S(1)} custom-call(s32[1,2304]{1,0:T(1,128)S(1)} %get-tuple-element.7.own_ref, s32[1,4608]{1,0:T(1,128)S(1)} %constant_dynamic-update-slice_fusion.near_ref, s32[1,4608]{1,0:T(1,128)S(1)} %collective-permute-done.2.far_ref, f32[64,2304]{1,0:T(8,128)S(1)} %copy-done.2, f32[64,2304]{1,0:T(8,128)S(1)} %collective-permute-done.3.head_far_ref, ...), custom_call_target="tpu_custom_call" | custom-call | tf_op jit(solution)/shard_map/score/pallas_call | solution.py:293
  17.2 12.8 %all_to_all.5.parts_ref = f32[32,1,128]{2,1,0:T(1,128)S(1)} all-to-all(f32[32,1,128]{2,1,0:T(1,128)S(1)} %bitcast.3), channel_id=1, replica_groups=mesh['pose'=16,'chan'=2] {'pose','chan'}, dimensions={0} | all-to-all | bytes 32768 | tf_op jit(solution)/shard_map/all_to_all | solution.py:387
  30.0 0.7 %final_sums.1 = (f32[1]{0:T(128)}, f32[1]{0:T(128)}) custom-call(f32[32,1,128]{2,1,0:T(1,128)S(1)} %all_to_all.5.parts_ref), custom_call_target="tpu_custom_call" | custom-call | tf_op jit(solution)/shard_map/final_sums/pallas_call | solution.py:329
  (2 shorter events, 0.0 us)
Async XLA Ops:
  0.6 8.2 %copy-start = (bf16[27,256,128]{2,1,0:T(8,128)(2,1)S(1)}, bf16[27,256,128]{2,1,0:T(8,128)(2,1)}, u32[]{:S(2)}) copy-start(bf16[27,256,128]{2,1,0:T(8,128)(2,1)} %weight2_ref.1) | copy-start | bytes 5308420
  1.5 5.8 %collective-permute-start.1 = (s32[1,2304]{1,0:T(1,128)S(1)}, s32[1,2304]{1,0:T(1,128)S(1)}, u32[]{:S(2)}, u32[]{:S(2)}) collective-permute-start(s32[1,2304]{1,0:T(1,128)S(1)} %get-tuple-element.7.own_ref), channel_id=1, source_target_pairs={{0,1},{1,3},{2,0},{3,5},{4,2},{5,7},{6,4},{7,9},{8,6},{9,11},{10,8... | collective-permute-start | bytes 27656 | tf_op jit(solution)/shard_map/ppermute | solution.py:363
  2.1 5.6 %collective-permute-start = (s32[1,2304]{1,0:T(1,128)S(1)}, s32[1,2304]{1,0:T(1,128)S(1)}, u32[]{:S(2)}, u32[]{:S(2)}) collective-permute-start(s32[1,2304]{1,0:T(1,128)S(1)} %get-tuple-element.7.own_ref), channel_id=1, source_target_pairs={{0,1},{1,5},{2,3},{3,7},{4,0},{5,9},{6,2},{7,11},{8,4},{9,13},{10,... | collective-permute-start | bytes 27656 | tf_op jit(solution)/shard_map/ppermute | solution.py:363
  4.1 4.7 %collective-permute-start.3 = (f32[64,2304]{1,0:T(8,128)}, f32[64,2304]{1,0:T(8,128)S(1)}, u32[]{:S(2)}, u32[]{:S(2)}) collective-permute-start(f32[64,2304]{1,0:T(8,128)} %head_own_ref.1), channel_id=1, source_target_pairs={{0,1},{1,0},{2,3},{3,2},{4,5},{5,4},{6,7},{7,6},{8,9},{9,8},{10,11... | collective-permute-start | bytes 1769480 | tf_op jit(solution)/shard_map/ppermute | solution.py:372
  5.4 1.5 %copy-start.1 = (bf16[27,128,256]{2,1,0:T(8,128)(2,1)S(1)}, bf16[27,128,256]{2,1,0:T(8,128)(2,1)}, u32[]{:S(2)}) copy-start(bf16[27,128,256]{2,1,0:T(8,128)(2,1)} %weight_ref.1) | copy-start | bytes 5308420
  6.8 2.0 %copy-start.2 = (f32[64,2304]{1,0:T(8,128)S(1)}, f32[64,2304]{1,0:T(8,128)}, u32[]{:S(2)}) copy-start(f32[64,2304]{1,0:T(8,128)} %head_own_ref.1) | copy-start | bytes 1769476
  6.8 2.0 %copy-start.3 = (f32[256]{0:T(256)S(1)}, f32[256]{0:T(256)}, u32[]{:S(2)}) copy-start(f32[256]{0:T(256)} %param.12) | copy-start | bytes 3076
  6.8 2.0 %copy-start.4 = (f32[128]{0:T(128)S(1)}, f32[128]{0:T(128)}, u32[]{:S(2)}) copy-start(f32[128]{0:T(128)} %param.14) | copy-start | bytes 1540
  7.7 1.2 %collective-permute-start.2 = (s32[1,4608]{1,0:T(1,128)S(1)}, s32[1,4608]{1,0:T(1,128)S(1)}, u32[]{:S(2)}, u32[]{:S(2)}) collective-permute-start(s32[1,4608]{1,0:T(1,128)S(1)} %constant_dynamic-update-slice_fusion.near_ref), channel_id=1, source_target_pairs={{0,1},{1,0},{2,3},{3,2},{4,5},{5,4},{6,7},{7,6},{8,9},{9,8},{10,11... | collective-permute-start | bytes 55304 | tf_op jit(solution)/shard_map/ppermute | solution.py:371

commit v4 on v3

--- a/solution.py
+++ b/solution.py
@@ -70,6 +70,7 @@
             pltpu.SemaphoreType.DMA((3,)),
         ],
         compiler_params=params(1),
+        cost_estimate=pl.CostEstimate(flops=4 * 10**9, bytes_accessed=8 << 20, transcendentals=0),
         name="encode",
     )(in_hbm(atom_type), in_hbm(occupancy), in_hbm(atom_embed))
 
@@ -129,13 +130,6 @@
                 count = jnp.where(own, count, 0.0)
         groups.append(jnp.where(kind == number, count, 0.0))
     return jnp.concatenate(groups, axis=0)
-
-
-def position(pose_total):
-    chan = lax.axis_index("chan")
-    block = lax.axis_index("pose") // pose_total
-    behind = jnp.where(chan == 1, block, XPLANES - 1 - block)
-    return chan, behind, [jnp.where(chan == 1, dx, 2 - dx) for dx in range(3)]
 
 
 def tap_rows(planes_ref, rows, chan, padded, types):
@@ -171,11 +165,11 @@
     ).astype(bf16).T
 
 
-def hidden_rows(operands, bias1, folded_ref, order, first, size, half_cells, chan, plane_ok):
+def hidden_rows(operands, bias1, folded_ref, first, size, half_cells, chan, plane_ok):
     total = bias1
     for dx in range(3):
         total = total + jnp.dot(
-            operands[dx](first, size), folded_ref[order[dx]], preferred_element_type=f32
+            operands[dx](first, size), folded_ref[dx], preferred_element_type=f32
         )
     index = first + lax.broadcasted_iota(jnp.int32, (size, 1), 0)
     lowest = jnp.where(plane_ok, jnp.where(chan == 0, SIDE, 0), half_cells + 2 * SIDE)
@@ -207,7 +201,8 @@
     sums_ref,
     head_ref,
 ):
-    chan, behind, order = position(pose_total)
+    chan = lax.axis_index("chan")
+    block = lax.axis_index("pose") // pose_total
     plane_cells = own_ref.shape[1]
     half_cells = plane_cells // 2
     padded = hot_ref.shape[1]
@@ -219,17 +214,24 @@
         :, head_cells
     ]
     near, far = near_ref[...], far_ref[...]
-    rows = [
-        jnp.where(behind >= 2, near[:, plane_cells:], 0),
-        jnp.where(behind >= 1, near[:, :plane_cells], 0),
-        own_ref[...],
-        jnp.where(behind <= XPLANES - 2, far[:, :plane_cells], 0),
-        jnp.where(behind <= XPLANES - 3, far[:, plane_cells:], 0),
-    ]
+    sides = []
+    for step in (1, 2):
+        cells = slice((step - 1) * plane_cells, step * plane_cells)
+        end = (block < step) | (block >= XPLANES - step)
+        above = (chan == lax.rem(block // step, 2)) != end
+        sides.append(
+            (
+                jnp.where(block >= step, jnp.where(above, far[:, cells], near[:, cells]), 0),
+                jnp.where(
+                    block < XPLANES - step, jnp.where(above, near[:, cells], far[:, cells]), 0
+                ),
+            )
+        )
+    rows = [sides[1][0], sides[0][0], own_ref[...], sides[0][1], sides[1][1]]
     plain, split = tap_rows(planes_ref, rows, chan, padded, types)
     bias1 = bias1_ref[...]
     operands = [reader(hot_ref, x) for x in range(5)]
-    plane_ok = [behind >= 1, True, behind <= XPLANES - 2]
+    plane_ok = [block >= 1, True, block <= XPLANES - 2]
     for first in range(0, padded, TILE):
         size = min(TILE, used - first)
         for x in range(5):
@@ -237,7 +239,7 @@
             if x >= 2:
                 h = x - 2
                 hidden_ref[h, first:first + size, :] = hidden_rows(
-                    operands[h:], bias1, folded_ref, order, first, size, half_cells, chan, plane_ok[h]
+                    operands[h:], bias1, folded_ref, first, size, half_cells, chan, plane_ok[h]
                 )
 
     width = weight2_ref.shape[2]
@@ -246,7 +248,7 @@
     def taps(first, size, *numbers):
         total = None
         for h in range(3):
-            weights = [weight2_ref[order[h] * 9 + tap] for tap in numbers]
+            weights = [weight2_ref[h * 9 + tap] for tap in numbers]
             part = jnp.dot(
                 hidden[h](first, size),
                 jnp.concatenate(weights, axis=1),
@@ -353,13 +355,18 @@
     pose_total = pose_count // XPLANES
     swap = [(0, 1), (1, 0)]
 
-    def fetch(steps):
-        by = steps * pose_total
+    def fetch(step):
         pairs = []
         for i in range(pose_count):
-            up = 2 * (i + by) + 1 if i + by < pose_count else 2 * i
-            down = 2 * (i - by) if i >= by else 2 * i + 1
-            pairs += [(2 * i, down), (2 * i + 1, up)]
+            above = i // pose_total // step % 2
+            sources = {}
+            for core, other in ((above, i + step * pose_total), (1 - above, i - step * pose_total)):
+                if 0 <= other < pose_count:
+                    sources[core] = 2 * other + core
+            for core in (0, 1):
+                if core not in sources:
+                    sources[core], sources[1 - core] = sources[1 - core], 2 * i + core
+            pairs += [(sources[core], 2 * i + core) for core in (0, 1)]
         return lax.ppermute(code, ("pose", "chan"), pairs)
 
     types = atom_embed.shape[0]

time: 30.9 us -> 29.6 us (0.958)
  local copies, waits for them, and re-layouts: 1.5 us -> 0.04 us
  blocking collectives: 12.8 us -> 11.7 us
  starting transfers between devices: 3.82 us -> 4.62 us
  waiting for transfers between devices: 1.54 us -> 2 us
    ppermute x2, starting transfers between devices: 2.58 us -> 4.54 us  [fetch(): return lax.ppermute(code, ('pose', 'chan'), pairs)]
    unnamed x11, local copies, waits for them, and re-layouts: 1.49 us -> 0.03 us
    ppermute x1, starting transfers between devices: 1.24 us -> 0.01 us  [on_device(): head_far = lax.ppermute(head_weight, 'chan', swap)]
    all_to_all x1, blocking collectives: 12.8 us -> 11.7 us  [on_device(): parts = lax.all_to_all(part[:, None, :], ('pose', 'chan'), 0, 0, tiled=True)]
    ppermute x2, waiting for transfers between devices: 0.35 us -> 0.89 us  [fetch(): return lax.ppermute(code, ('pose', 'chan'), pairs)]
  transfers between devices with their start and end apart: 4 -> 4, of which waited for: 2 -> 2; matrix products, arithmetic and copies ran while one was open for 0% -> 0% of each run, Pallas kernels for 1% -> 2%
where the time goes in v4:
time: 29.6 us; the launch traced here: 29.4 us
  blocking collectives  11.7 us (40%)
  Pallas kernels  10.3 us (35%)
  starting transfers between devices  4.62 us (16%)
  waiting for transfers between devices  2 us (7%)
  between operations  0.72 us (2%)
    all_to_all x1, blocking collectives, on_device(): parts = lax.all_to_all(part[:, None, :], ('pose', 'chan'), 0, 0, tiled=True)  11.7 us
    pallas_call x1, Pallas kernels, score(): pl.pallas_call(functools.partial(score_kernel, pose_total, types), out_sh...  8.29 us
    ppermute x2, starting transfers between devices, fetch(): return lax.ppermute(code, ('pose', 'chan'), pairs)  4.54 us
    ppermute x1, waiting for transfers between devices, on_device(): far = lax.ppermute(near, 'chan', swap)  1.1 us
    pallas_call x1, Pallas kernels, encode(): pl.pallas_call(encode_kernel, out_shape=(pltpu.VMEM(atom_type.shape, jnp....  0.91 us
    ppermute x2, waiting for transfers between devices, fetch(): return lax.ppermute(code, ('pose', 'chan'), pairs)  0.89 us
    pallas_call x1, Pallas kernels, final_sums(): pl.pallas_call(functools.partial(final_kernel, pose_total, chan_count), o...  0.66 us
  transfers between devices with their start and end apart: 4, of which 2 were waited for; matrix products, arithmetic and copies ran while one was open for 0% of the time, Pallas kernels for 2%

profile of v4, /device:TPU:0, one launch (start us, length us, event | category | flops | bytes accessed | tf_op | source)
XLA Modules:
  0.0 29.4 jit_solution(10437970007276227542)
XLA Ops:
  0.6 0.0 copy-start.2
  0.6 0.0 copy-start.1
  0.7 0.9 %encode.1 = (s32[1,2304]{1,0:T(1,128)S(1)}, f32[64,128]{1,0:T(8,128)S(1)}) custom-call(s32[1,2304]{1,0:T(1,128)} %type_hbm.1, s32[1,2304]{1,0:T(1,128)} %count_hbm.1, bf16[28,128]{1,0:T(8,128)(2,1)} %embed_hbm.1), custom_call_target="tpu_custom_call" | custom-call | flops 4000000000 | bytes 8388608 | tf_op jit(solution)/shard_map/encode/pallas_call | solution.py:59
  1.6 0.0 copy-start
  1.6 0.0 copy-start.3
  1.6 0.0 copy-start.4
  1.6 3.0 %collective-permute-start.1 = (s32[1,2304]{1,0:T(1,128)S(1)}, s32[1,2304]{1,0:T(1,128)S(1)}, u32[]{:S(2)}, u32[]{:S(2)}) collective-permute-start(s32[1,2304]{1,0:T(1,128)S(1)} %get-tuple-element.7.own_ref), channel_id=1, source_target_pairs={{1,0},{2,1},{0,2},{5,3},{6,4},{3,5},{4,6},{9,7},{10,8},{7,9},{8,10... | collective-permute-start | bytes 27656 | tf_op jit(solution)/shard_map/ppermute | solution.py:370
  4.6 1.5 %collective-permute-start = (s32[1,2304]{1,0:T(1,128)S(1)}, s32[1,2304]{1,0:T(1,128)S(1)}, u32[]{:S(2)}, u32[]{:S(2)}) collective-permute-start(s32[1,2304]{1,0:T(1,128)S(1)} %get-tuple-element.7.own_ref), channel_id=1, source_target_pairs={{1,0},{4,1},{3,2},{6,3},{0,4},{9,5},{2,6},{11,7},{12,8},{5,9},{14,... | collective-permute-start | bytes 27656 | tf_op jit(solution)/shard_map/ppermute | solution.py:370
  6.1 0.0 copy-done.2
  6.1 0.0 collective-permute-start.3
  6.1 0.0 copy-done.1
  6.2 0.5 %fold_embedding.1.folded_ref = bf16[3,768,256]{2,1,0:T(8,128)(2,1)S(1)} custom-call(f32[64,128]{1,0:T(8,128)S(1)} %get-tuple-element.8.pair_ref, bf16[27,128,256]{2,1,0:T(8,128)(2,1)S(1)} %copy-done.1), custom_call_target="tpu_custom_call" | custom-call | tf_op jit(solution)/shard_map/fold_embedding/pallas_call | solution.py:98
  6.6 0.0 collective-permute-done.1
  6.6 0.9 %collective-permute-done = s32[1,2304]{1,0:T(1,128)S(1)} collective-permute-done((s32[1,2304]{1,0:T(1,128)S(1)}, s32[1,2304]{1,0:T(1,128)S(1)}, u32[]{:S(2)}, u32[]{:S(2)}) %collective-permute-start) | collective-permute-done | bytes 9248 | tf_op jit(solution)/shard_map/ppermute | solution.py:370
  7.5 0.1 collective-permute-start.2
  7.6 1.1 %collective-permute-done.2.far_ref = s32[1,4608]{1,0:T(1,128)S(1)} collective-permute-done((s32[1,4608]{1,0:T(1,128)S(1)}, s32[1,4608]{1,0:T(1,128)S(1)}, u32[]{:S(2)}, u32[]{:S(2)}) %collective-permute-start.2) | collective-permute-done | bytes 18464 | tf_op jit(solution)/shard_map/ppermute | solution.py:378
  8.7 0.0 collective-permute-done.3.head_far_ref
  8.7 0.0 copy-done
  8.7 0.0 copy-done.3
  8.7 0.0 copy-done.4
  8.7 8.3 %score.1 = f32[32,128]{1,0:T(8,128)S(1)} custom-call(s32[1,2304]{1,0:T(1,128)S(1)} %get-tuple-element.7.own_ref, s32[1,4608]{1,0:T(1,128)S(1)} %constant_dynamic-update-slice_fusion.near_ref, s32[1,4608]{1,0:T(1,128)S(1)} %collective-permute-done.2.far_ref, f32[64,2304]{1,0:T(8,128)S(1)} %copy-done.2, f32[64,2304]{1,0:T(8,128)S(1)} %collective-permute-done.3.head_far_ref, ...), custom_call_target="tpu_custom_call" | custom-call | tf_op jit(solution)/shard_map/score/pallas_call | solution.py:295
  17.0 11.7 %all_to_all.5.parts_ref = f32[32,1,128]{2,1,0:T(1,128)S(1)} all-to-all(f32[32,1,128]{2,1,0:T(1,128)S(1)} %bitcast.3), channel_id=1, replica_groups=mesh['pose'=16,'chan'=2] {'pose','chan'}, dimensions={0} | all-to-all | bytes 32768 | tf_op jit(solution)/shard_map/all_to_all | solution.py:394
  28.8 0.7 %final_sums.1 = (f32[1]{0:T(128)}, f32[1]{0:T(128)}) custom-call(f32[32,1,128]{2,1,0:T(1,128)S(1)} %all_to_all.5.parts_ref), custom_call_target="tpu_custom_call" | custom-call | tf_op jit(solution)/shard_map/final_sums/pallas_call | solution.py:331
  (2 shorter events, 0.0 us)
Async XLA Ops:
  0.6 5.5 %copy-start.2 = (f32[64,2304]{1,0:T(8,128)S(1)}, f32[64,2304]{1,0:T(8,128)}, u32[]{:S(2)}) copy-start(f32[64,2304]{1,0:T(8,128)} %head_own_ref.1) | copy-start | bytes 1769476
  0.6 5.5 %copy-start.1 = (bf16[27,128,256]{2,1,0:T(8,128)(2,1)S(1)}, bf16[27,128,256]{2,1,0:T(8,128)(2,1)}, u32[]{:S(2)}) copy-start(bf16[27,128,256]{2,1,0:T(8,128)(2,1)} %weight_ref.1) | copy-start | bytes 5308420
  1.6 7.2 %copy-start = (bf16[27,256,128]{2,1,0:T(8,128)(2,1)S(1)}, bf16[27,256,128]{2,1,0:T(8,128)(2,1)}, u32[]{:S(2)}) copy-start(bf16[27,256,128]{2,1,0:T(8,128)(2,1)} %weight2_ref.1) | copy-start | bytes 5308420
  1.6 7.1 %copy-start.3 = (f32[256]{0:T(256)S(1)}, f32[256]{0:T(256)}, u32[]{:S(2)}) copy-start(f32[256]{0:T(256)} %param.12) | copy-start | bytes 3076
  1.6 7.1 %copy-start.4 = (f32[128]{0:T(128)S(1)}, f32[128]{0:T(128)}, u32[]{:S(2)}) copy-start(f32[128]{0:T(128)} %param.14) | copy-start | bytes 1540
  1.6 5.0 %collective-permute-start.1 = (s32[1,2304]{1,0:T(1,128)S(1)}, s32[1,2304]{1,0:T(1,128)S(1)}, u32[]{:S(2)}, u32[]{:S(2)}) collective-permute-start(s32[1,2304]{1,0:T(1,128)S(1)} %get-tuple-element.7.own_ref), channel_id=1, source_target_pairs={{1,0},{2,1},{0,2},{5,3},{6,4},{3,5},{4,6},{9,7},{10,8},{7,9},{8,10... | collective-permute-start | bytes 27656 | tf_op jit(solution)/shard_map/ppermute | solution.py:370
  4.6 2.9 %collective-permute-start = (s32[1,2304]{1,0:T(1,128)S(1)}, s32[1,2304]{1,0:T(1,128)S(1)}, u32[]{:S(2)}, u32[]{:S(2)}) collective-permute-start(s32[1,2304]{1,0:T(1,128)S(1)} %get-tuple-element.7.own_ref), channel_id=1, source_target_pairs={{1,0},{4,1},{3,2},{6,3},{0,4},{9,5},{2,6},{11,7},{12,8},{5,9},{14,... | collective-permute-start | bytes 27656 | tf_op jit(solution)/shard_map/ppermute | solution.py:370
  6.1 2.6 %collective-permute-start.3 = (f32[64,2304]{1,0:T(8,128)S(1)}, f32[64,2304]{1,0:T(8,128)S(1)}, u32[]{:S(2)}, u32[]{:S(2)}) collective-permute-start(f32[64,2304]{1,0:T(8,128)S(1)} %copy-done.2), channel_id=1, source_target_pairs={{0,1},{1,0},{2,3},{3,2},{4,5},{5,4},{6,7},{7,6},{8,9},{9,8},{10,11... | collective-permute-start | bytes 1769480 | tf_op jit(solution)/shard_map/ppermute | solution.py:379
  7.5 1.2 %collective-permute-start.2 = (s32[1,4608]{1,0:T(1,128)S(1)}, s32[1,4608]{1,0:T(1,128)S(1)}, u32[]{:S(2)}, u32[]{:S(2)}) collective-permute-start(s32[1,4608]{1,0:T(1,128)S(1)} %constant_dynamic-update-slice_fusion.near_ref), channel_id=1, source_target_pairs={{0,1},{1,0},{2,3},{3,2},{4,5},{5,4},{6,7},{7,6},{8,9},{9,8},{10,11... | collective-permute-start | bytes 55304 | tf_op jit(solution)/shard_map/ppermute | solution.py:378

commit v5 on v4

--- a/solution.py
+++ b/solution.py
@@ -10,8 +10,8 @@
 SIDE = 48
 XPLANES = 16
 LANES = 128
-TILE = 256
-PARTS = 3
+TILE = 640
+STEP = 1152
 TAPS = [(shift_y, shift_z) for shift_y in (-1, 0, 1) for shift_z in (-1, 0, 1)]
 
 bf16 = jnp.bfloat16
@@ -105,30 +105,27 @@
 
 
 def one_hot(rows, x, types, start):
-    width = TILE
-    depth = round_up(types * len(rows), LANES)
-    sub = lax.broadcasted_iota(jnp.int32, (8, 1), 0)
+    shape = (16, TILE)
+    sub = lax.broadcasted_iota(jnp.int32, shape, 0).astype(f32).astype(bf16)
+    empty = jnp.zeros(shape, bf16)
 
     def spread(row):
-        return jnp.broadcast_to(row[x:x + 1, start:start + width], (8, width))
-
+        return jnp.broadcast_to(row[x:x + 1, start:start + TILE], shape).astype(bf16)
+
+    kinds = [spread(kind) for kind, _ in rows]
+    counts = [spread(count) for _, count in rows]
     groups = []
-    for first in range(0, depth, 8):
-        low, high = first // types, (first + 7) // types
+    for first in range(0, round_up(types * len(rows), LANES), 16):
+        low, high = first // types, (first + 15) // types
         if low >= len(rows):
-            groups.append(jnp.zeros((8, width), f32))
+            groups.append(empty)
             continue
-        kind, count = spread(rows[low][0]), spread(rows[low][1])
-        number = sub + (first - types * low)
-        if high != low:
-            own = sub < types * high - first
-            number = jnp.where(own, number, number - types)
-            if high < len(rows):
-                kind = jnp.where(own, kind, spread(rows[high][0]))
-                count = jnp.where(own, count, spread(rows[high][1]))
-            else:
-                count = jnp.where(own, count, 0.0)
-        groups.append(jnp.where(kind == number, count, 0.0))
+        group = jnp.where(kinds[low] == sub + bf16(first - types * low), counts[low], empty)
+        if high != low and high < len(rows):
+            group = jnp.where(
+                kinds[high] == sub + bf16(first - types * high), counts[high], group
+            )
+        groups.append(group)
     return jnp.concatenate(groups, axis=0)
 
 
@@ -149,10 +146,10 @@
         moved = jnp.where(inside, moved, 0)
         kind = lax.shift_right_logical(moved, 2)
         count = moved & 3
-        plain.append((kind, count.astype(f32)))
+        plain.append((kind.astype(f32), count.astype(f32)))
         split.append(
             (
-                jnp.where(count == 3, kind + types, kind),
+                jnp.where(count == 3, kind + types, kind).astype(f32),
                 jnp.where(count == 3, 1, count).astype(f32),
             )
         )
@@ -162,7 +159,7 @@
 def both_hot(plain, split, x, types, first):
     return jnp.concatenate(
         [one_hot(plain, x, types, first), one_hot(split, x, 2 * types, first)], axis=0
-    ).astype(bf16).T
+    ).T
 
 
 def hidden_rows(operands, bias1, folded_ref, first, size, half_cells, chan, plane_ok):
@@ -257,33 +254,26 @@
             total = part if total is None else total + part
         return [total[:, n * width:(n + 1) * width] for n in range(len(numbers))]
 
-    ends = [(0, half_cells), (0, half_cells + SIDE), (SIDE, half_cells + SIDE), (2 * SIDE, used), (2 * SIDE, used)]
-    for pair, (begin, end) in enumerate(ends):
-        size = (end - begin) // PARTS
-        numbers = [2 * pair, 2 * pair + 1][: 2 if pair < 4 else 1]
-        for first in range(begin, end, size):
-            for number, value in zip(numbers, taps(first, size, *numbers)):
-                sums_ref[number, 8 + first:8 + first + size, :] = value
     bias2 = bias2_ref[...]
+    step = STEP
+    column = lax.rem(lax.broadcasted_iota(jnp.int32, (step, 1), 0), SIDE)
     running = jnp.zeros((8, width), f32)
-    for first in range(0, half_cells, LANES):
-        moved = []
-        for shift_z in range(3):
-            offset = 8 + first + shift_z - 1
-            moved.append(
-                sums_ref[shift_z, offset:offset + LANES, :]
-                + sums_ref[3 + shift_z, offset + SIDE:offset + SIDE + LANES, :]
-                + sums_ref[6 + shift_z, offset + 2 * SIDE:offset + 2 * SIDE + LANES, :]
-            )
-        column = lax.rem(first + lax.broadcasted_iota(jnp.int32, (LANES, 1), 0), SIDE)
+    for first in range(0, half_cells, step):
+        tap0, tap1 = taps(first, step, 0, 1)
+        tap2, tap3 = taps(first, step + SIDE, 2, 3)
+        tap4, tap5 = taps(first + SIDE, step, 4, 5)
+        tap6, tap7 = taps(first + 2 * SIDE, step, 6, 7)
+        (tap8,) = taps(first + 2 * SIDE, step, 8)
+        sums_ref[0, 8 + first:8 + first + step, :] = tap0 + tap3[SIDE:] + tap6
+        middle = bias2 + tap1 + tap4 + tap7
+        sums_ref[1, 8 + first:8 + first + step, :] = tap2[:step] + tap5 + tap8
         mapped = (
-            bias2
-            + moved[1]
-            + jnp.where(column > 0, moved[0], 0.0)
-            + jnp.where(column < SIDE - 1, moved[2], 0.0)
-        )
-        scored = jnp.maximum(mapped, 0.0) * head_ref[:, first:first + LANES].T
-        running = running + jnp.sum(scored.reshape(LANES // 8, 8, width), axis=0)
+            middle
+            + jnp.where(column > 0, sums_ref[0, 7 + first:7 + first + step, :], 0.0)
+            + jnp.where(column < SIDE - 1, sums_ref[1, 9 + first:9 + first + step, :], 0.0)
+        )
+        scored = jnp.maximum(mapped, 0.0) * head_ref[:, first:first + step].T
+        running = running + jnp.sum(scored.reshape(step // 8, 8, width), axis=0)
     out_ref[...] = jnp.broadcast_to(jnp.sum(running), out_ref.shape)
 
 
@@ -299,7 +289,7 @@
             pltpu.VMEM((8, plane_cells + 3 * LANES), jnp.int32),
             pltpu.VMEM((5, padded, depth), bf16),
             pltpu.VMEM((3, padded, mid), bf16),
-            pltpu.VMEM((9, padded + 16, width), f32),
+            pltpu.VMEM((2, plane_cells // 2 + 16, width), f32),
             pltpu.VMEM((width, plane_cells // 2), f32),
         ],
         compiler_params=params(40),

time: 29.6 us -> 29 us (0.980)
  Pallas kernels: 10.3 us -> 9.68 us
    pallas_call x1, Pallas kernels: 8.29 us -> 7.65 us  [score(): pl.pallas_call(functools.partial(score_kernel, pose_total, types), out_sh...]
where the time goes in v5:
time: 29 us; the launch traced here: 28.8 us
  blocking collectives  11.7 us (40%)
  Pallas kernels  9.68 us (33%)
  starting transfers between devices  4.62 us (16%)
  waiting for transfers between devices  2 us (7%)
  between operations  0.72 us (2%)
    all_to_all x1, blocking collectives, on_device(): parts = lax.all_to_all(part[:, None, :], ('pose', 'chan'), 0, 0, tiled=True)  11.7 us
    pallas_call x1, Pallas kernels, score(): pl.pallas_call(functools.partial(score_kernel, pose_total, types), out_sh...  7.65 us
    ppermute x2, starting transfers between devices, fetch(): return lax.ppermute(code, ('pose', 'chan'), pairs)  4.54 us
    ppermute x1, waiting for transfers between devices, on_device(): far = lax.ppermute(near, 'chan', swap)  1.1 us
    pallas_call x1, Pallas kernels, encode(): pl.pallas_call(encode_kernel, out_shape=(pltpu.VMEM(atom_type.shape, jnp....  0.91 us
    ppermute x2, waiting for transfers between devices, fetch(): return lax.ppermute(code, ('pose', 'chan'), pairs)  0.89 us
    pallas_call x1, Pallas kernels, final_sums(): pl.pallas_call(functools.partial(final_kernel, pose_total, chan_count), o...  0.66 us
  transfers between devices with their start and end apart: 4, of which 2 were waited for; matrix products, arithmetic and copies ran while one was open for 0% of the time, Pallas kernels for 2%

profile of v5, /device:TPU:0, one launch (start us, length us, event | category | flops | bytes accessed | tf_op | source)
XLA Modules:
  0.0 28.8 jit_solution(495202804232207840)
XLA Ops:
  0.6 0.0 copy-start.2
  0.6 0.0 copy-start.1
  0.7 0.9 %encode.1 = (s32[1,2304]{1,0:T(1,128)S(1)}, f32[64,128]{1,0:T(8,128)S(1)}) custom-call(s32[1,2304]{1,0:T(1,128)} %type_hbm.1, s32[1,2304]{1,0:T(1,128)} %count_hbm.1, bf16[28,128]{1,0:T(8,128)(2,1)} %embed_hbm.1), custom_call_target="tpu_custom_call" | custom-call | flops 4000000000 | bytes 8388608 | tf_op jit(solution)/shard_map/encode/pallas_call | solution.py:59
  1.6 0.0 copy-start
  1.6 0.0 copy-start.3
  1.6 0.0 copy-start.4
  1.6 3.0 %collective-permute-start.1 = (s32[1,2304]{1,0:T(1,128)S(1)}, s32[1,2304]{1,0:T(1,128)S(1)}, u32[]{:S(2)}, u32[]{:S(2)}) collective-permute-start(s32[1,2304]{1,0:T(1,128)S(1)} %get-tuple-element.7.own_ref), channel_id=1, source_target_pairs={{1,0},{2,1},{0,2},{5,3},{6,4},{3,5},{4,6},{9,7},{10,8},{7,9},{8,10... | collective-permute-start | bytes 27656 | tf_op jit(solution)/shard_map/ppermute | solution.py:360
  4.6 1.5 %collective-permute-start = (s32[1,2304]{1,0:T(1,128)S(1)}, s32[1,2304]{1,0:T(1,128)S(1)}, u32[]{:S(2)}, u32[]{:S(2)}) collective-permute-start(s32[1,2304]{1,0:T(1,128)S(1)} %get-tuple-element.7.own_ref), channel_id=1, source_target_pairs={{1,0},{4,1},{3,2},{6,3},{0,4},{9,5},{2,6},{11,7},{12,8},{5,9},{14,... | collective-permute-start | bytes 27656 | tf_op jit(solution)/shard_map/ppermute | solution.py:360
  6.1 0.0 copy-done.2
  6.1 0.0 collective-permute-start.3
  6.1 0.0 copy-done.1
  6.2 0.5 %fold_embedding.1.folded_ref = bf16[3,768,256]{2,1,0:T(8,128)(2,1)S(1)} custom-call(f32[64,128]{1,0:T(8,128)S(1)} %get-tuple-element.8.pair_ref, bf16[27,128,256]{2,1,0:T(8,128)(2,1)S(1)} %copy-done.1), custom_call_target="tpu_custom_call" | custom-call | tf_op jit(solution)/shard_map/fold_embedding/pallas_call | solution.py:98
  6.6 0.0 collective-permute-done.1
  6.6 0.9 %collective-permute-done = s32[1,2304]{1,0:T(1,128)S(1)} collective-permute-done((s32[1,2304]{1,0:T(1,128)S(1)}, s32[1,2304]{1,0:T(1,128)S(1)}, u32[]{:S(2)}, u32[]{:S(2)}) %collective-permute-start) | collective-permute-done | bytes 9248 | tf_op jit(solution)/shard_map/ppermute | solution.py:360
  7.5 0.1 collective-permute-start.2
  7.6 1.1 %collective-permute-done.2.far_ref = s32[1,4608]{1,0:T(1,128)S(1)} collective-permute-done((s32[1,4608]{1,0:T(1,128)S(1)}, s32[1,4608]{1,0:T(1,128)S(1)}, u32[]{:S(2)}, u32[]{:S(2)}) %collective-permute-start.2) | collective-permute-done | bytes 18464 | tf_op jit(solution)/shard_map/ppermute | solution.py:368
  8.7 0.0 collective-permute-done.3.head_far_ref
  8.7 0.0 copy-done
  8.7 0.0 copy-done.3
  8.7 0.0 copy-done.4
  8.7 7.6 %score.1 = f32[32,128]{1,0:T(8,128)S(1)} custom-call(s32[1,2304]{1,0:T(1,128)S(1)} %get-tuple-element.7.own_ref, s32[1,4608]{1,0:T(1,128)S(1)} %constant_dynamic-update-slice_fusion.near_ref, s32[1,4608]{1,0:T(1,128)S(1)} %collective-permute-done.2.far_ref, f32[64,2304]{1,0:T(8,128)S(1)} %copy-done.2, f32[64,2304]{1,0:T(8,128)S(1)} %collective-permute-done.3.head_far_ref, ...), custom_call_target="tpu_custom_call" | custom-call | tf_op jit(solution)/shard_map/score/pallas_call | solution.py:285
  16.4 11.7 %all_to_all.5.parts_ref = f32[32,1,128]{2,1,0:T(1,128)S(1)} all-to-all(f32[32,1,128]{2,1,0:T(1,128)S(1)} %bitcast.3), channel_id=1, replica_groups=mesh['pose'=16,'chan'=2] {'pose','chan'}, dimensions={0} | all-to-all | bytes 32768 | tf_op jit(solution)/shard_map/all_to_all | solution.py:384
  28.1 0.7 %final_sums.1 = (f32[1]{0:T(128)}, f32[1]{0:T(128)}) custom-call(f32[32,1,128]{2,1,0:T(1,128)S(1)} %all_to_all.5.parts_ref), custom_call_target="tpu_custom_call" | custom-call | tf_op jit(solution)/shard_map/final_sums/pallas_call | solution.py:321
  (2 shorter events, 0.0 us)
Async XLA Ops:
  0.6 5.5 %copy-start.2 = (f32[64,2304]{1,0:T(8,128)S(1)}, f32[64,2304]{1,0:T(8,128)}, u32[]{:S(2)}) copy-start(f32[64,2304]{1,0:T(8,128)} %head_own_ref.1) | copy-start | bytes 1769476
  0.6 5.5 %copy-start.1 = (bf16[27,128,256]{2,1,0:T(8,128)(2,1)S(1)}, bf16[27,128,256]{2,1,0:T(8,128)(2,1)}, u32[]{:S(2)}) copy-start(bf16[27,128,256]{2,1,0:T(8,128)(2,1)} %weight_ref.1) | copy-start | bytes 5308420
  1.6 7.2 %copy-start = (bf16[27,256,128]{2,1,0:T(8,128)(2,1)S(1)}, bf16[27,256,128]{2,1,0:T(8,128)(2,1)}, u32[]{:S(2)}) copy-start(bf16[27,256,128]{2,1,0:T(8,128)(2,1)} %weight2_ref.1) | copy-start | bytes 5308420
  1.6 7.1 %copy-start.3 = (f32[256]{0:T(256)S(1)}, f32[256]{0:T(256)}, u32[]{:S(2)}) copy-start(f32[256]{0:T(256)} %param.12) | copy-start | bytes 3076
  1.6 7.1 %copy-start.4 = (f32[128]{0:T(128)S(1)}, f32[128]{0:T(128)}, u32[]{:S(2)}) copy-start(f32[128]{0:T(128)} %param.14) | copy-start | bytes 1540
  1.6 5.0 %collective-permute-start.1 = (s32[1,2304]{1,0:T(1,128)S(1)}, s32[1,2304]{1,0:T(1,128)S(1)}, u32[]{:S(2)}, u32[]{:S(2)}) collective-permute-start(s32[1,2304]{1,0:T(1,128)S(1)} %get-tuple-element.7.own_ref), channel_id=1, source_target_pairs={{1,0},{2,1},{0,2},{5,3},{6,4},{3,5},{4,6},{9,7},{10,8},{7,9},{8,10... | collective-permute-start | bytes 27656 | tf_op jit(solution)/shard_map/ppermute | solution.py:360
  4.6 2.9 %collective-permute-start = (s32[1,2304]{1,0:T(1,128)S(1)}, s32[1,2304]{1,0:T(1,128)S(1)}, u32[]{:S(2)}, u32[]{:S(2)}) collective-permute-start(s32[1,2304]{1,0:T(1,128)S(1)} %get-tuple-element.7.own_ref), channel_id=1, source_target_pairs={{1,0},{4,1},{3,2},{6,3},{0,4},{9,5},{2,6},{11,7},{12,8},{5,9},{14,... | collective-permute-start | bytes 27656 | tf_op jit(solution)/shard_map/ppermute | solution.py:360
  6.1 2.6 %collective-permute-start.3 = (f32[64,2304]{1,0:T(8,128)S(1)}, f32[64,2304]{1,0:T(8,128)S(1)}, u32[]{:S(2)}, u32[]{:S(2)}) collective-permute-start(f32[64,2304]{1,0:T(8,128)S(1)} %copy-done.2), channel_id=1, source_target_pairs={{0,1},{1,0},{2,3},{3,2},{4,5},{5,4},{6,7},{7,6},{8,9},{9,8},{10,11... | collective-permute-start | bytes 1769480 | tf_op jit(solution)/shard_map/ppermute | solution.py:369
  7.5 1.2 %collective-permute-start.2 = (s32[1,4608]{1,0:T(1,128)S(1)}, s32[1,4608]{1,0:T(1,128)S(1)}, u32[]{:S(2)}, u32[]{:S(2)}) collective-permute-start(s32[1,4608]{1,0:T(1,128)S(1)} %constant_dynamic-update-slice_fusion.near_ref), channel_id=1, source_target_pairs={{0,1},{1,0},{2,3},{3,2},{4,5},{5,4},{6,7},{7,6},{8,9},{9,8},{10,11... | collective-permute-start | bytes 55304 | tf_op jit(solution)/shard_map/ppermute | solution.py:368

commit v6 on v5

--- a/solution.py
+++ b/solution.py
@@ -34,49 +34,41 @@
     return pltpu.CompilerParams(vmem_limit_bytes=megabytes << 20)
 
 
-def encode_kernel(type_hbm, count_hbm, embed_hbm, code_ref, pair_ref, type_ref, count_ref, embed_ref, sems):
-    types = embed_ref.shape[0]
-    half = pair_ref.shape[0] // 2
+def encode_kernel(type_hbm, count_hbm, code_ref, type_ref, count_ref, sems):
     copies = [
         pltpu.make_async_copy(source, target, sems.at[n])
-        for n, (source, target) in enumerate(
-            ((type_hbm, type_ref), (count_hbm, count_ref), (embed_hbm, embed_ref))
-        )
+        for n, (source, target) in enumerate(((type_hbm, type_ref), (count_hbm, count_ref)))
     ]
     for copy in copies:
         copy.start()
-    pair_ref[...] = jnp.zeros_like(pair_ref)
     for copy in copies:
         copy.wait()
     code_ref[...] = type_ref[...] * 4 + count_ref[...]
-    embed = embed_ref[...].astype(f32)
-    pair_ref[:types, :] = embed
-    pair_ref[half:half + types, :] = (3.0 * embed).astype(bf16).astype(f32)
-
-
-def encode(atom_type, occupancy, atom_embed):
-    types, width = atom_embed.shape
+
+
+def encode(atom_type, occupancy):
     return pl.pallas_call(
         encode_kernel,
-        out_shape=(
-            pltpu.VMEM(atom_type.shape, jnp.int32),
-            pltpu.VMEM((2 * round_up(types, 16), width), f32),
-        ),
-        in_specs=[pl.BlockSpec(memory_space=pl.ANY)] * 3,
+        out_shape=pltpu.VMEM(atom_type.shape, jnp.int32),
+        in_specs=[pl.BlockSpec(memory_space=pl.ANY)] * 2,
         scratch_shapes=[
             pltpu.VMEM(atom_type.shape, jnp.int32),
             pltpu.VMEM(atom_type.shape, jnp.int32),
-            pltpu.VMEM(atom_embed.shape, bf16),
-            pltpu.SemaphoreType.DMA((3,)),
+            pltpu.SemaphoreType.DMA((2,)),
         ],
         compiler_params=params(1),
         cost_estimate=pl.CostEstimate(flops=4 * 10**9, bytes_accessed=8 << 20, transcendentals=0),
         name="encode",
-    )(in_hbm(atom_type), in_hbm(occupancy), in_hbm(atom_embed))
-
-
-def fold_kernel(types, pair_ref, weight_ref, folded_ref, rows_ref):
+    )(in_hbm(atom_type), in_hbm(occupancy))
+
+
+def fold_kernel(embed_ref, weight_ref, folded_ref, pair_ref, rows_ref):
+    types = embed_ref.shape[0]
     half = pair_ref.shape[0] // 2
+    embed = embed_ref[...].astype(f32)
+    pair_ref[...] = jnp.zeros_like(pair_ref)
+    pair_ref[:types, :] = embed
+    pair_ref[half:half + types, :] = (3.0 * embed).astype(bf16).astype(f32)
     rest = round_up(9 * types, LANES)
     pair = pair_ref[...].astype(bf16)
     rows_ref[...] = jnp.zeros_like(rows_ref)
@@ -92,16 +84,20 @@
         folded_ref[dx] = rows_ref[dx].astype(bf16)
 
 
-def fold_embedding(types, pair, conv1_weight):
+def fold_embedding(atom_embed, conv1_weight):
+    types, width = atom_embed.shape
     mid = conv1_weight.shape[2]
     depth = round_up(9 * types, LANES) + round_up(18 * types, LANES)
     return pl.pallas_call(
-        functools.partial(fold_kernel, types),
+        fold_kernel,
         out_shape=pltpu.VMEM((3, depth, mid), bf16),
-        scratch_shapes=[pltpu.VMEM((3, depth, mid), f32)],
+        scratch_shapes=[
+            pltpu.VMEM((2 * round_up(types, 16), width), f32),
+            pltpu.VMEM((3, depth, mid), f32),
+        ],
         compiler_params=params(12),
         name="fold_embedding",
-    )(in_vmem(pair), in_vmem(conv1_weight))
+    )(in_vmem(atom_embed), in_vmem(conv1_weight))
 
 
 def one_hot(rows, x, types, start):
@@ -360,9 +356,9 @@
         return lax.ppermute(code, ("pose", "chan"), pairs)
 
     types = atom_embed.shape[0]
-    code, pair = encode(atom_type, occupancy, atom_embed)
+    code = encode(atom_type, occupancy)
     second, first, folded = lax.optimization_barrier(
-        (fetch(2), fetch(1), fold_embedding(types, pair, conv1_weight))
+        (fetch(2), fetch(1), fold_embedding(atom_embed, conv1_weight))
     )
     near = jnp.concatenate([first, second], axis=1)
     far = lax.ppermute(near, "chan", swap)

time: 29 us -> 29 us (level)
  no operation moved by 1% of the time
where the time goes in v6:
time: 29 us; the launch traced here: 28.8 us
  blocking collectives  11.7 us (40%)
  Pallas kernels  9.66 us (33%)
  starting transfers between devices  4.62 us (16%)
  waiting for transfers between devices  1.99 us (7%)
  between operations  0.74 us (3%)
    all_to_all x1, blocking collectives, on_device(): parts = lax.all_to_all(part[:, None, :], ('pose', 'chan'), 0, 0, tiled=True)  11.7 us
    pallas_call x1, Pallas kernels, score(): pl.pallas_call(functools.partial(score_kernel, pose_total, types), out_sh...  7.65 us
    ppermute x2, starting transfers between devices, fetch(): return lax.ppermute(code, ('pose', 'chan'), pairs)  4.54 us
    ppermute x1, waiting for transfers between devices, on_device(): far = lax.ppermute(near, 'chan', swap)  1.1 us
    pallas_call x1, Pallas kernels, encode(): pl.pallas_call(encode_kernel, out_shape=pltpu.VMEM(atom_type.shape, jnp.i...  0.89 us
    ppermute x2, waiting for transfers between devices, fetch(): return lax.ppermute(code, ('pose', 'chan'), pairs)  0.88 us
    pallas_call x1, Pallas kernels, final_sums(): pl.pallas_call(functools.partial(final_kernel, pose_total, chan_count), o...  0.66 us
  transfers between devices with their start and end apart: 4, of which 2 were waited for; matrix products, arithmetic and copies ran while one was open for 0% of the time, Pallas kernels for 2%

profile of v6, /device:TPU:0, one launch (start us, length us, event | category | flops | bytes accessed | tf_op | source)
XLA Modules:
  0.0 28.8 jit_solution(654016631454412781)
XLA Ops:
  0.6 0.0 copy-start.2
  0.6 0.0 copy-start.1
  0.7 0.0 copy-start.3
  0.7 0.9 %encode.1.own_ref = s32[1,2304]{1,0:T(1,128)S(1)} custom-call(s32[1,2304]{1,0:T(1,128)} %type_hbm.1, s32[1,2304]{1,0:T(1,128)} %count_hbm.1), custom_call_target="tpu_custom_call" | custom-call | flops 4000000000 | bytes 8388608 | tf_op jit(solution)/shard_map/encode/pallas_call | solution.py:50
  1.6 0.0 copy-start
  1.6 0.0 copy-start.4
  1.6 0.0 copy-start.5
  1.6 3.0 %collective-permute-start.1 = (s32[1,2304]{1,0:T(1,128)S(1)}, s32[1,2304]{1,0:T(1,128)S(1)}, u32[]{:S(2)}, u32[]{:S(2)}) collective-permute-start(s32[1,2304]{1,0:T(1,128)S(1)} %encode.1.own_ref), channel_id=1, source_target_pairs={{1,0},{2,1},{0,2},{5,3},{6,4},{3,5},{4,6},{9,7},{10,8},{7,9},{8,10... | collective-permute-start | bytes 27656 | tf_op jit(solution)/shard_map/ppermute | solution.py:356
  4.6 1.5 %collective-permute-start = (s32[1,2304]{1,0:T(1,128)S(1)}, s32[1,2304]{1,0:T(1,128)S(1)}, u32[]{:S(2)}, u32[]{:S(2)}) collective-permute-start(s32[1,2304]{1,0:T(1,128)S(1)} %encode.1.own_ref), channel_id=1, source_target_pairs={{1,0},{4,1},{3,2},{6,3},{0,4},{9,5},{2,6},{11,7},{12,8},{5,9},{14,... | collective-permute-start | bytes 27656 | tf_op jit(solution)/shard_map/ppermute | solution.py:356
  6.1 0.0 copy-done.2
  6.1 0.0 collective-permute-start.3
  6.1 0.0 copy-done.1
  6.1 0.0 copy-done.3
  6.1 0.5 %fold_embedding.1.folded_ref = bf16[3,768,256]{2,1,0:T(8,128)(2,1)S(1)} custom-call(bf16[28,128]{1,0:T(8,128)(2,1)S(1)} %copy-done.3, bf16[27,128,256]{2,1,0:T(8,128)(2,1)S(1)} %copy-done.1), custom_call_target="tpu_custom_call" | custom-call | tf_op jit(solution)/shard_map/fold_embedding/pallas_call | solution.py:91
  6.6 0.0 collective-permute-done.1
  6.6 0.9 %collective-permute-done = s32[1,2304]{1,0:T(1,128)S(1)} collective-permute-done((s32[1,2304]{1,0:T(1,128)S(1)}, s32[1,2304]{1,0:T(1,128)S(1)}, u32[]{:S(2)}, u32[]{:S(2)}) %collective-permute-start) | collective-permute-done | bytes 9248 | tf_op jit(solution)/shard_map/ppermute | solution.py:356
  7.5 0.1 collective-permute-start.2
  7.6 1.1 %collective-permute-done.2.far_ref = s32[1,4608]{1,0:T(1,128)S(1)} collective-permute-done((s32[1,4608]{1,0:T(1,128)S(1)}, s32[1,4608]{1,0:T(1,128)S(1)}, u32[]{:S(2)}, u32[]{:S(2)}) %collective-permute-start.2) | collective-permute-done | bytes 18464 | tf_op jit(solution)/shard_map/ppermute | solution.py:364
  8.7 0.0 collective-permute-done.3.head_far_ref
  8.7 0.0 copy-done
  8.7 0.0 copy-done.4
  8.7 0.0 copy-done.5
  8.7 7.6 %score.1 = f32[32,128]{1,0:T(8,128)S(1)} custom-call(s32[1,2304]{1,0:T(1,128)S(1)} %encode.1.own_ref, s32[1,4608]{1,0:T(1,128)S(1)} %constant_dynamic-update-slice_fusion.near_ref, s32[1,4608]{1,0:T(1,128)S(1)} %collective-permute-done.2.far_ref, f32[64,2304]{1,0:T(8,128)S(1)} %copy-done.2, f32[64,2304]{1,0:T(8,128)S(1)} %collective-permute-done.3.head_far_ref, ...), custom_call_target="tpu_custom_call" | custom-call | tf_op jit(solution)/shard_map/score/pallas_call | solution.py:281
  16.4 11.7 %all_to_all.5.parts_ref = f32[32,1,128]{2,1,0:T(1,128)S(1)} all-to-all(f32[32,1,128]{2,1,0:T(1,128)S(1)} %bitcast.3), channel_id=1, replica_groups=mesh['pose'=16,'chan'=2] {'pose','chan'}, dimensions={0} | all-to-all | bytes 32768 | tf_op jit(solution)/shard_map/all_to_all | solution.py:380
  28.1 0.7 %final_sums.1 = (f32[1]{0:T(128)}, f32[1]{0:T(128)}) custom-call(f32[32,1,128]{2,1,0:T(1,128)S(1)} %all_to_all.5.parts_ref), custom_call_target="tpu_custom_call" | custom-call | tf_op jit(solution)/shard_map/final_sums/pallas_call | solution.py:317
  (2 shorter events, 0.0 us)
Async XLA Ops:
  0.6 5.5 %copy-start.2 = (f32[64,2304]{1,0:T(8,128)S(1)}, f32[64,2304]{1,0:T(8,128)}, u32[]{:S(2)}) copy-start(f32[64,2304]{1,0:T(8,128)} %head_own_ref.1) | copy-start | bytes 1769476
  0.6 5.5 %copy-start.1 = (bf16[27,128,256]{2,1,0:T(8,128)(2,1)S(1)}, bf16[27,128,256]{2,1,0:T(8,128)(2,1)}, u32[]{:S(2)}) copy-start(bf16[27,128,256]{2,1,0:T(8,128)(2,1)} %weight_ref.1) | copy-start | bytes 5308420
  0.7 5.5 %copy-start.3 = (bf16[28,128]{1,0:T(8,128)(2,1)S(1)}, bf16[28,128]{1,0:T(8,128)(2,1)}, u32[]{:S(2)}) copy-start(bf16[28,128]{1,0:T(8,128)(2,1)} %embed_ref.1) | copy-start | bytes 21508
  1.6 7.2 %copy-start = (bf16[27,256,128]{2,1,0:T(8,128)(2,1)S(1)}, bf16[27,256,128]{2,1,0:T(8,128)(2,1)}, u32[]{:S(2)}) copy-start(bf16[27,256,128]{2,1,0:T(8,128)(2,1)} %weight2_ref.1) | copy-start | bytes 5308420
  1.6 7.1 %copy-start.4 = (f32[256]{0:T(256)S(1)}, f32[256]{0:T(256)}, u32[]{:S(2)}) copy-start(f32[256]{0:T(256)} %param.12) | copy-start | bytes 3076
  1.6 7.1 %copy-start.5 = (f32[128]{0:T(128)S(1)}, f32[128]{0:T(128)}, u32[]{:S(2)}) copy-start(f32[128]{0:T(128)} %param.14) | copy-start | bytes 1540
  1.6 5.0 %collective-permute-start.1 = (s32[1,2304]{1,0:T(1,128)S(1)}, s32[1,2304]{1,0:T(1,128)S(1)}, u32[]{:S(2)}, u32[]{:S(2)}) collective-permute-start(s32[1,2304]{1,0:T(1,128)S(1)} %encode.1.own_ref), channel_id=1, source_target_pairs={{1,0},{2,1},{0,2},{5,3},{6,4},{3,5},{4,6},{9,7},{10,8},{7,9},{8,10... | collective-permute-start | bytes 27656 | tf_op jit(solution)/shard_map/ppermute | solution.py:356
  4.6 2.9 %collective-permute-start = (s32[1,2304]{1,0:T(1,128)S(1)}, s32[1,2304]{1,0:T(1,128)S(1)}, u32[]{:S(2)}, u32[]{:S(2)}) collective-permute-start(s32[1,2304]{1,0:T(1,128)S(1)} %encode.1.own_ref), channel_id=1, source_target_pairs={{1,0},{4,1},{3,2},{6,3},{0,4},{9,5},{2,6},{11,7},{12,8},{5,9},{14,... | collective-permute-start | bytes 27656 | tf_op jit(solution)/shard_map/ppermute | solution.py:356
  6.1 2.6 %collective-permute-start.3 = (f32[64,2304]{1,0:T(8,128)S(1)}, f32[64,2304]{1,0:T(8,128)S(1)}, u32[]{:S(2)}, u32[]{:S(2)}) collective-permute-start(f32[64,2304]{1,0:T(8,128)S(1)} %copy-done.2), channel_id=1, source_target_pairs={{0,1},{1,0},{2,3},{3,2},{4,5},{5,4},{6,7},{7,6},{8,9},{9,8},{10,11... | collective-permute-start | bytes 1769480 | tf_op jit(solution)/shard_map/ppermute | solution.py:365
  7.5 1.2 %collective-permute-start.2 = (s32[1,4608]{1,0:T(1,128)S(1)}, s32[1,4608]{1,0:T(1,128)S(1)}, u32[]{:S(2)}, u32[]{:S(2)}) collective-permute-start(s32[1,4608]{1,0:T(1,128)S(1)} %constant_dynamic-update-slice_fusion.near_ref), channel_id=1, source_target_pairs={{0,1},{1,0},{2,3},{3,2},{4,5},{5,4},{6,7},{7,6},{8,9},{9,8},{10,11... | collective-permute-start | bytes 55304 | tf_op jit(solution)/shard_map/ppermute | solution.py:364
